TPU v7x, 32 devices: a whole 2x2x4 slice. The times are simulated.
32 devices in a mesh: grp: 2 (over y), shot: 4 (over x, core), slab: 4 (over z).
Axes of the slice: x: 2, y: 2, z: 4, core: 2. Of those that a mesh axis runs over, the one named last changes fastest.
Arguments:
- courant_sq: float32 [512, 1024], P(('grp', 'slab')), parts along dimension 0, may hold values from 0.05 to 0.25
- sponge_level: int32 [512, 1024], P(('grp', 'slab')), parts along dimension 0, may hold values from 0 to 3
- source_later: float32 [16, 256, 1024], P(('grp', 'shot'), 'slab'), parts along dimension 0, may hold values from -6 to 6
- source_now: float32 [16, 256, 1024], P(('grp', 'shot'), 'slab'), parts along dimension 0, may hold values from -6 to 6
- receiver_later: float32 [16, 256, 1024], P(('grp', 'shot'), 'slab'), parts along dimension 0, may hold values from -6 to 6
- receiver_now: float32 [16, 256, 1024], P(('grp', 'shot'), 'slab'), parts along dimension 0, may hold values from -6 to 6
- traces: float32 [16, 16, 512], P(('grp', 'shot')), parts along dimension 0, may hold values from -24 to 24
- wavelet: float32 [512], P('grp'), parts along dimension 0, may hold values from -24 to 24
- source_depth: int32 [16], P(('grp', 'shot')), parts along dimension 0, may hold values from 0 to 255
- source_lateral: int32 [16], P(('grp', 'shot')), parts along dimension 0, may hold values from 0 to 1023
- receiver_depth: int32 [16, 512], P(('grp', 'shot')), parts along dimension 0, may hold values from 0 to 255
- receiver_lateral: int32 [16, 512], P(('grp', 'shot')), parts along dimension 0, may hold values from 0 to 1023
- checkpoint_step: int32 [16], P(('grp', 'shot')), parts along dimension 0, may hold values from 0 to 240
Outputs:
- image: float32 [512, 1024], P(('grp', 'slab')), parts along dimension 0
- source_out: float32 [16, 256, 1024], P(('grp', 'shot'), 'slab'), parts along dimension 0
- receiver_out: float32 [16, 256, 1024], P(('grp', 'shot'), 'slab'), parts along dimension 0
There are 2 independent parts, one for each index of `grp`. A program takes and returns all parts, laid end to end along the dimension named above; each array names one. Nothing has to cross between parts.
All inputs are finite; a program needn't handle non-finite values.
Results may differ from a plain program's by a relative error of at most 0.0003.
Values sent between devices are 32-bit elements; how exact they have to be, the bound alone decides.
A program may use at most 64 MiB of HBM per device.

v0:
```python
import math
import jax
import jax.numpy as jnp
from jax import lax
from jax.sharding import PartitionSpec as P

STEPS = 16
stencil_coeffs = (-205.0 / 72.0, 8.0 / 5.0, -1.0 / 5.0, 8.0 / 315.0, -1.0 / 560.0)


def extended_2(cells, sides, width):
    for axis, dim in sides:
        count = lax.axis_size(axis)
        ends = count - 1
        head = lax.slice_in_dim(cells, 0, width, axis=dim)
        tail = lax.slice_in_dim(cells, cells.shape[dim] - width, cells.shape[dim], axis=dim)
        cells = jnp.concatenate(
            [
                lax.ppermute(tail, axis, [(i, (i + 1) % count) for i in range(ends)]),
                cells,
                lax.ppermute(head, axis, [((i + 1) % count, i) for i in range(ends)]),
            ],
            axis=dim,
        )
    return cells


def laplace(extended):
    row_count = extended.shape[-2] - 8
    width = extended.shape[-1]
    centre = extended[..., 4 : 4 + row_count, :]
    pad_spec = [(0, 0)] * (centre.ndim - 1) + [(4, 4)]
    padded = jnp.pad(centre, pad_spec)
    result = 2.0 * stencil_coeffs[0] * centre
    for offset in range(1, 5):
        result = result + stencil_coeffs[offset] * (
            extended[..., 4 + offset : 4 + offset + row_count, :]
            + extended[..., 4 - offset : 4 - offset + row_count, :]
            + padded[..., 4 + offset : 4 + offset + width]
            + padded[..., 4 - offset : 4 - offset + width]
        )
    return result


def local(
    courant_sq,
    sponge_level,
    source_later,
    source_now,
    receiver_later,
    receiver_now,
    traces,
    wavelet,
    source_depth,
    source_lateral,
    receiver_depth,
    receiver_lateral,
    checkpoint_step,
):
    slab_rows = courant_sq.shape[0]
    lateral_cells = courant_sq.shape[1]
    first_row = lax.axis_index("slab") * slab_rows
    damping = 1.0 - 0.06 * sponge_level.astype(jnp.float32)
    lateral_ids = jnp.arange(lateral_cells, dtype=jnp.int32)
    lateral_table = (receiver_lateral[:, :, None] == lateral_ids[None, None, :]).astype(jnp.float32)
    source_column = lateral_ids[None, :] == source_lateral[:, None]

    def advance(src_now, src_hi, rec_now, rec_hi, laplacian, velocity, damper, top_row, step_index):
        row_count = src_now.shape[1]
        row_ids = top_row + jnp.arange(row_count, dtype=jnp.int32)
        pulse = wavelet[checkpoint_step + STEPS - 1 - step_index]
        source_cell = (row_ids[None, :, None] == source_depth[:, None, None]) & source_column[
            :, None, :
        ]
        injected_src = jnp.where(source_cell, pulse[:, None, None], 0.0)
        src_next = 2.0 * src_now - src_hi + velocity * laplacian[0] - velocity * injected_src
        trace_now = lax.dynamic_index_in_dim(traces, step_index, 1, keepdims=False)
        depth_table = jnp.where(
            row_ids[None, :, None] == receiver_depth[:, None, :], trace_now[:, None, :], 0.0
        )
        injected_rec = jnp.einsum(
            "szr,srx->szx",
            depth_table,
            lateral_table,
            precision=lax.Precision.HIGHEST,
            preferred_element_type=jnp.float32,
        )
        rec_next = 2.0 * rec_now - rec_hi + velocity * laplacian[1] + velocity * injected_rec
        rec_next = damper * rec_next
        return (src_next, rec_next)

    start_image = jnp.zeros(courant_sq.shape, jnp.float32)
    model = extended_2(jnp.stack([courant_sq, damping]), (("slab", 1),), 8)
    velocity_wide = model[0, 4 : slab_rows + 12]
    damper_wide = model[1, 4 : slab_rows + 12]

    def pair_step(pair_index, carry):
        src_hi, src_now, rec_hi, rec_now, image_local = carry
        step_first = 2 * pair_index
        image_local = image_local + jnp.sum(src_now * rec_now, axis=0)
        extended = extended_2(jnp.stack([src_now, rec_now, src_hi, rec_hi]), (("slab", 2),), 8)
        laplacian = laplace(extended[0:2])
        src_wide = extended[0, :, 4 : slab_rows + 12]
        rec_wide = extended[1, :, 4 : slab_rows + 12]
        src_hi_wide = extended[2, :, 4 : slab_rows + 12]
        rec_hi_wide = extended[3, :, 4 : slab_rows + 12]
        src_mid, rec_mid = advance(
            src_wide,
            src_hi_wide,
            rec_wide,
            rec_hi_wide,
            laplacian,
            velocity_wide,
            damper_wide,
            first_row - 4,
            step_first,
        )
        src_centre = src_mid[:, 4 : slab_rows + 4]
        rec_centre = rec_mid[:, 4 : slab_rows + 4]
        image_local = image_local + jnp.sum(src_centre * rec_centre, axis=0)
        second = laplace(jnp.stack([src_mid, rec_mid]))
        src_last, rec_last = advance(
            src_centre,
            src_now,
            rec_centre,
            rec_now,
            second,
            courant_sq,
            damping,
            first_row,
            step_first + 1,
        )
        return (src_centre, src_last, rec_centre, rec_last, image_local)

    carry = lax.fori_loop(
        0,
        STEPS // 2,
        pair_step,
        (source_later, source_now, receiver_later, receiver_now, start_image),
    )
    source_final = carry[1]
    receiver_final = carry[3]
    image_total = lax.psum(carry[4], "shot")
    shots_all = lax.axis_size("shot") * source_now.shape[0]
    image = image_total / math.sqrt(STEPS * shots_all)
    return (image, source_final, receiver_final)


def solution(mesh):
    in_specs = (
        P(("grp", "slab"), None),
        P(("grp", "slab"), None),
        P(("grp", "shot"), "slab", None),
        P(("grp", "shot"), "slab", None),
        P(("grp", "shot"), "slab", None),
        P(("grp", "shot"), "slab", None),
        P(("grp", "shot"), None, None),
        P("grp"),
        P(("grp", "shot")),
        P(("grp", "shot")),
        P(("grp", "shot"), None),
        P(("grp", "shot"), None),
        P(("grp", "shot")),
    )
    out_specs = (
        P(("grp", "slab"), None),
        P(("grp", "shot"), "slab", None),
        P(("grp", "shot"), "slab", None),
    )
    return jax.shard_map(local, mesh=mesh, in_specs=in_specs, out_specs=out_specs, check_vma=False)
```

profile of v0, /device:TPU:0, one launch (start us, length us, event | category | flops | bytes accessed | tf_op | source)
XLA Modules:
  0.0 274.1 jit_solution(1386798049830185891)
XLA Ops:
  9.0 5.1 %collective-permute-start.2 = (f32[2,8,1024]{2,1,0:T(8,128)S(1)}, f32[2,8,1024]{2,1,0:T(8,128)S(1)}, u32[]{:S(2)}, u32[]{:S(2)}) collective-permute-start(f32[2,8,1024]{2,1,0:T(8,128)S(1)} %get-tuple-element.729), channel_id=1, source_target_pairs={{0,1},{1,2},{2,3},{4,5},{5,6},{6,7},{8,9},{9,10},{10,11},{12,13},{... | collective-permute-start | bytes 196616 | tf_op jit(solution)/shard_map/ppermute | solution.py:19
  16.0 4.3 %collective-permute-done.3 = f32[2,8,1024]{2,1,0:T(8,128)S(1)} collective-permute-done((f32[2,8,1024]{2,1,0:T(8,128)S(1)}, f32[2,8,1024]{2,1,0:T(8,128)S(1)}, u32[]{:S(2)}, u32[]{:S(2)}) %collective-permute-start.3) | collective-permute-done | bytes 65568 | tf_op jit(solution)/shard_map/ppermute | solution.py:21
  21.1 209.0 %while.26 = (s32[]{:T(128)}, f32[2,64,1024]{2,1,0:T(8,128)S(1)}, f32[2,64,1024]{2,1,0:T(8,128)S(1)}, f32[2,64,1024]{2,1,0:T(8,128)S(1)}, f32[2,64,1024]{2,1,0:T(...) while((s32[]{:T(128)}, f32[2,64,1024]{2,1,0:T(8,128)S(1)}, ...), condition=%wide.region_3.4_spmd.clone, body=%wide.region_0.3_spmd.clone.sunk | while | flops 1741394304 | bytes 51560036 | solution.py:135
  23.2 4.6 %collective-permute-start.1 = (f32[4,2,8,1024]{3,2,1,0:T(8,128)}, f32[4,2,8,1024]{3,2,1,0:T(8,128)S(1)}, u32[]{:S(2)}, u32[]{:S(2)}) collective-permute-start(f32[4,2,8,1024]{3,2,1,0:T(8,128)} %get-tuple-element.863), channel_id=1, source_target_pairs={{0,1},{1,2},{2,3},{4,5},{5,6},{6,7},{8,9},{9,10},{10,11},{12,13},{... | collective-permute-start | bytes 786440 | tf_op jit(solution)/shard_map/while/body/eval_jaxpr/ppermute | solution.py:19
  32.3 2.6 fusion.117
  35.9 3.2 %fusion.118 = f32[2,72,1024]{2,1,0:T(8,128)S(1)} fusion(f32[2,2,72,1024]{3,2,1,0:T(8,128)S(1)} %fusion.117, f32[4,2,80,1024]{3,2,1,0:T(8,128)S(1)} %pad_maximum_fusion.23, s32[2,512]{1,0:T(2,128)S(1)} %copy-done.17, f32[72,1024]{1,0:T(8,128)S(1)} %bitcast.101, f32[72,1024]{1,0:T(8,128)S(1)} %bitcast.98, f32[2,512]{1,0:T(2,128)S(1)} %get-tuple-element.864, ...), kind=kOutput, calls=%fused_computation.109.clone.1 | convolution fusion | flops 909246464 | bytes 2961696 | tf_op jit(solution)/shard_map/while/body/eval_jaxpr/szr,srx->szx/dot_general | solution.py:81
  39.2 2.4 fusion.121
  42.9 3.1 %fusion.122 = f32[2,64,1024]{2,1,0:T(8,128)S(1)} fusion(s32[2,512]{1,0:T(2,128)S(1)} %copy-done.17, f32[2,2,64,1024]{3,2,1,0:T(8,128)S(1)} %fusion.121, f32[2,64,1024]{2,1,0:T(8,128)S(1)} %get-tuple-element.904, f32[2,64,1024]{2,1,0:T(8,128)S(1)} %get-tuple-element.927, f32[64,1024]{1,0:T(8,128)S(1)} %copy-done.12, ...), kind=kOutput, calls=%fused_computation.39.clone.1 | convolution fusion | flops 808452096 | bytes 2633984 | tf_op jit(solution)/shard_map/while/body/eval_jaxpr/szr,srx->szx/dot_general | solution.py:81
  49.0 4.9 %collective-permute-start.1 = (f32[4,2,8,1024]{3,2,1,0:T(8,128)}, f32[4,2,8,1024]{3,2,1,0:T(8,128)S(1)}, u32[]{:S(2)}, u32[]{:S(2)}) collective-permute-start(f32[4,2,8,1024]{3,2,1,0:T(8,128)} %get-tuple-element.863), channel_id=1, source_target_pairs={{0,1},{1,2},{2,3},{4,5},{5,6},{6,7},{8,9},{9,10},{10,11},{12,13},{... | collective-permute-start | bytes 786440 | tf_op jit(solution)/shard_map/while/body/eval_jaxpr/ppermute | solution.py:19
  56.6 1.6 collective-permute-done.1
  58.5 2.6 fusion.117
  62.1 3.2 %fusion.118 = f32[2,72,1024]{2,1,0:T(8,128)S(1)} fusion(f32[2,2,72,1024]{3,2,1,0:T(8,128)S(1)} %fusion.117, f32[4,2,80,1024]{3,2,1,0:T(8,128)S(1)} %pad_maximum_fusion.23, s32[2,512]{1,0:T(2,128)S(1)} %copy-done.17, f32[72,1024]{1,0:T(8,128)S(1)} %bitcast.101, f32[72,1024]{1,0:T(8,128)S(1)} %bitcast.98, f32[2,512]{1,0:T(2,128)S(1)} %get-tuple-element.864, ...), kind=kOutput, calls=%fused_computation.109.clone.1 | convolution fusion | flops 909246464 | bytes 2961696 | tf_op jit(solution)/shard_map/while/body/eval_jaxpr/szr,srx->szx/dot_general | solution.py:81
  65.4 2.4 fusion.121
  69.1 3.1 %fusion.122 = f32[2,64,1024]{2,1,0:T(8,128)S(1)} fusion(s32[2,512]{1,0:T(2,128)S(1)} %copy-done.17, f32[2,2,64,1024]{3,2,1,0:T(8,128)S(1)} %fusion.121, f32[2,64,1024]{2,1,0:T(8,128)S(1)} %get-tuple-element.904, f32[2,64,1024]{2,1,0:T(8,128)S(1)} %get-tuple-element.927, f32[64,1024]{1,0:T(8,128)S(1)} %copy-done.12, ...), kind=kOutput, calls=%fused_computation.39.clone.1 | convolution fusion | flops 808452096 | bytes 2633984 | tf_op jit(solution)/shard_map/while/body/eval_jaxpr/szr,srx->szx/dot_general | solution.py:81
  75.2 4.9 %collective-permute-start.1 = (f32[4,2,8,1024]{3,2,1,0:T(8,128)}, f32[4,2,8,1024]{3,2,1,0:T(8,128)S(1)}, u32[]{:S(2)}, u32[]{:S(2)}) collective-permute-start(f32[4,2,8,1024]{3,2,1,0:T(8,128)} %get-tuple-element.863), channel_id=1, source_target_pairs={{0,1},{1,2},{2,3},{4,5},{5,6},{6,7},{8,9},{9,10},{10,11},{12,13},{... | collective-permute-start | bytes 786440 | tf_op jit(solution)/shard_map/while/body/eval_jaxpr/ppermute | solution.py:19
  82.8 1.6 collective-permute-done.1
  84.7 2.6 fusion.117
  88.3 3.2 %fusion.118 = f32[2,72,1024]{2,1,0:T(8,128)S(1)} fusion(f32[2,2,72,1024]{3,2,1,0:T(8,128)S(1)} %fusion.117, f32[4,2,80,1024]{3,2,1,0:T(8,128)S(1)} %pad_maximum_fusion.23, s32[2,512]{1,0:T(2,128)S(1)} %copy-done.17, f32[72,1024]{1,0:T(8,128)S(1)} %bitcast.101, f32[72,1024]{1,0:T(8,128)S(1)} %bitcast.98, f32[2,512]{1,0:T(2,128)S(1)} %get-tuple-element.864, ...), kind=kOutput, calls=%fused_computation.109.clone.1 | convolution fusion | flops 909246464 | bytes 2961696 | tf_op jit(solution)/shard_map/while/body/eval_jaxpr/szr,srx->szx/dot_general | solution.py:81
  91.6 2.4 fusion.121
  95.2 3.1 %fusion.122 = f32[2,64,1024]{2,1,0:T(8,128)S(1)} fusion(s32[2,512]{1,0:T(2,128)S(1)} %copy-done.17, f32[2,2,64,1024]{3,2,1,0:T(8,128)S(1)} %fusion.121, f32[2,64,1024]{2,1,0:T(8,128)S(1)} %get-tuple-element.904, f32[2,64,1024]{2,1,0:T(8,128)S(1)} %get-tuple-element.927, f32[64,1024]{1,0:T(8,128)S(1)} %copy-done.12, ...), kind=kOutput, calls=%fused_computation.39.clone.1 | convolution fusion | flops 808452096 | bytes 2633984 | tf_op jit(solution)/shard_map/while/body/eval_jaxpr/szr,srx->szx/dot_general | solution.py:81
  101.4 4.9 %collective-permute-start.1 = (f32[4,2,8,1024]{3,2,1,0:T(8,128)}, f32[4,2,8,1024]{3,2,1,0:T(8,128)S(1)}, u32[]{:S(2)}, u32[]{:S(2)}) collective-permute-start(f32[4,2,8,1024]{3,2,1,0:T(8,128)} %get-tuple-element.863), channel_id=1, source_target_pairs={{0,1},{1,2},{2,3},{4,5},{5,6},{6,7},{8,9},{9,10},{10,11},{12,13},{... | collective-permute-start | bytes 786440 | tf_op jit(solution)/shard_map/while/body/eval_jaxpr/ppermute | solution.py:19
  110.8 2.6 fusion.117
  114.4 3.2 %fusion.118 = f32[2,72,1024]{2,1,0:T(8,128)S(1)} fusion(f32[2,2,72,1024]{3,2,1,0:T(8,128)S(1)} %fusion.117, f32[4,2,80,1024]{3,2,1,0:T(8,128)S(1)} %pad_maximum_fusion.23, s32[2,512]{1,0:T(2,128)S(1)} %copy-done.17, f32[72,1024]{1,0:T(8,128)S(1)} %bitcast.101, f32[72,1024]{1,0:T(8,128)S(1)} %bitcast.98, f32[2,512]{1,0:T(2,128)S(1)} %get-tuple-element.864, ...), kind=kOutput, calls=%fused_computation.109.clone.1 | convolution fusion | flops 909246464 | bytes 2961696 | tf_op jit(solution)/shard_map/while/body/eval_jaxpr/szr,srx->szx/dot_general | solution.py:81
  117.8 2.4 fusion.121
  121.4 3.1 %fusion.122 = f32[2,64,1024]{2,1,0:T(8,128)S(1)} fusion(s32[2,512]{1,0:T(2,128)S(1)} %copy-done.17, f32[2,2,64,1024]{3,2,1,0:T(8,128)S(1)} %fusion.121, f32[2,64,1024]{2,1,0:T(8,128)S(1)} %get-tuple-element.904, f32[2,64,1024]{2,1,0:T(8,128)S(1)} %get-tuple-element.927, f32[64,1024]{1,0:T(8,128)S(1)} %copy-done.12, ...), kind=kOutput, calls=%fused_computation.39.clone.1 | convolution fusion | flops 808452096 | bytes 2633984 | tf_op jit(solution)/shard_map/while/body/eval_jaxpr/szr,srx->szx/dot_general | solution.py:81
  127.6 4.9 %collective-permute-start.1 = (f32[4,2,8,1024]{3,2,1,0:T(8,128)}, f32[4,2,8,1024]{3,2,1,0:T(8,128)S(1)}, u32[]{:S(2)}, u32[]{:S(2)}) collective-permute-start(f32[4,2,8,1024]{3,2,1,0:T(8,128)} %get-tuple-element.863), channel_id=1, source_target_pairs={{0,1},{1,2},{2,3},{4,5},{5,6},{6,7},{8,9},{9,10},{10,11},{12,13},{... | collective-permute-start | bytes 786440 | tf_op jit(solution)/shard_map/while/body/eval_jaxpr/ppermute | solution.py:19
  137.0 2.6 fusion.117
  140.6 3.2 %fusion.118 = f32[2,72,1024]{2,1,0:T(8,128)S(1)} fusion(f32[2,2,72,1024]{3,2,1,0:T(8,128)S(1)} %fusion.117, f32[4,2,80,1024]{3,2,1,0:T(8,128)S(1)} %pad_maximum_fusion.23, s32[2,512]{1,0:T(2,128)S(1)} %copy-done.17, f32[72,1024]{1,0:T(8,128)S(1)} %bitcast.101, f32[72,1024]{1,0:T(8,128)S(1)} %bitcast.98, f32[2,512]{1,0:T(2,128)S(1)} %get-tuple-element.864, ...), kind=kOutput, calls=%fused_computation.109.clone.1 | convolution fusion | flops 909246464 | bytes 2961696 | tf_op jit(solution)/shard_map/while/body/eval_jaxpr/szr,srx->szx/dot_general | solution.py:81
  143.9 2.4 fusion.121
  147.6 3.1 %fusion.122 = f32[2,64,1024]{2,1,0:T(8,128)S(1)} fusion(s32[2,512]{1,0:T(2,128)S(1)} %copy-done.17, f32[2,2,64,1024]{3,2,1,0:T(8,128)S(1)} %fusion.121, f32[2,64,1024]{2,1,0:T(8,128)S(1)} %get-tuple-element.904, f32[2,64,1024]{2,1,0:T(8,128)S(1)} %get-tuple-element.927, f32[64,1024]{1,0:T(8,128)S(1)} %copy-done.12, ...), kind=kOutput, calls=%fused_computation.39.clone.1 | convolution fusion | flops 808452096 | bytes 2633984 | tf_op jit(solution)/shard_map/while/body/eval_jaxpr/szr,srx->szx/dot_general | solution.py:81
  153.7 4.9 %collective-permute-start.1 = (f32[4,2,8,1024]{3,2,1,0:T(8,128)}, f32[4,2,8,1024]{3,2,1,0:T(8,128)S(1)}, u32[]{:S(2)}, u32[]{:S(2)}) collective-permute-start(f32[4,2,8,1024]{3,2,1,0:T(8,128)} %get-tuple-element.863), channel_id=1, source_target_pairs={{0,1},{1,2},{2,3},{4,5},{5,6},{6,7},{8,9},{9,10},{10,11},{12,13},{... | collective-permute-start | bytes 786440 | tf_op jit(solution)/shard_map/while/body/eval_jaxpr/ppermute | solution.py:19
  163.2 2.6 fusion.117
  166.8 3.2 %fusion.118 = f32[2,72,1024]{2,1,0:T(8,128)S(1)} fusion(f32[2,2,72,1024]{3,2,1,0:T(8,128)S(1)} %fusion.117, f32[4,2,80,1024]{3,2,1,0:T(8,128)S(1)} %pad_maximum_fusion.23, s32[2,512]{1,0:T(2,128)S(1)} %copy-done.17, f32[72,1024]{1,0:T(8,128)S(1)} %bitcast.101, f32[72,1024]{1,0:T(8,128)S(1)} %bitcast.98, f32[2,512]{1,0:T(2,128)S(1)} %get-tuple-element.864, ...), kind=kOutput, calls=%fused_computation.109.clone.1 | convolution fusion | flops 909246464 | bytes 2961696 | tf_op jit(solution)/shard_map/while/body/eval_jaxpr/szr,srx->szx/dot_general | solution.py:81
  170.1 2.4 fusion.121
  173.8 3.1 %fusion.122 = f32[2,64,1024]{2,1,0:T(8,128)S(1)} fusion(s32[2,512]{1,0:T(2,128)S(1)} %copy-done.17, f32[2,2,64,1024]{3,2,1,0:T(8,128)S(1)} %fusion.121, f32[2,64,1024]{2,1,0:T(8,128)S(1)} %get-tuple-element.904, f32[2,64,1024]{2,1,0:T(8,128)S(1)} %get-tuple-element.927, f32[64,1024]{1,0:T(8,128)S(1)} %copy-done.12, ...), kind=kOutput, calls=%fused_computation.39.clone.1 | convolution fusion | flops 808452096 | bytes 2633984 | tf_op jit(solution)/shard_map/while/body/eval_jaxpr/szr,srx->szx/dot_general | solution.py:81
  179.9 4.9 %collective-permute-start.1 = (f32[4,2,8,1024]{3,2,1,0:T(8,128)}, f32[4,2,8,1024]{3,2,1,0:T(8,128)S(1)}, u32[]{:S(2)}, u32[]{:S(2)}) collective-permute-start(f32[4,2,8,1024]{3,2,1,0:T(8,128)} %get-tuple-element.863), channel_id=1, source_target_pairs={{0,1},{1,2},{2,3},{4,5},{5,6},{6,7},{8,9},{9,10},{10,11},{12,13},{... | collective-permute-start | bytes 786440 | tf_op jit(solution)/shard_map/while/body/eval_jaxpr/ppermute | solution.py:19
  189.4 2.6 fusion.117
  193.0 3.2 %fusion.118 = f32[2,72,1024]{2,1,0:T(8,128)S(1)} fusion(f32[2,2,72,1024]{3,2,1,0:T(8,128)S(1)} %fusion.117, f32[4,2,80,1024]{3,2,1,0:T(8,128)S(1)} %pad_maximum_fusion.23, s32[2,512]{1,0:T(2,128)S(1)} %copy-done.17, f32[72,1024]{1,0:T(8,128)S(1)} %bitcast.101, f32[72,1024]{1,0:T(8,128)S(1)} %bitcast.98, f32[2,512]{1,0:T(2,128)S(1)} %get-tuple-element.864, ...), kind=kOutput, calls=%fused_computation.109.clone.1 | convolution fusion | flops 909246464 | bytes 2961696 | tf_op jit(solution)/shard_map/while/body/eval_jaxpr/szr,srx->szx/dot_general | solution.py:81
  196.3 2.4 fusion.121
  199.9 3.1 %fusion.122 = f32[2,64,1024]{2,1,0:T(8,128)S(1)} fusion(s32[2,512]{1,0:T(2,128)S(1)} %copy-done.17, f32[2,2,64,1024]{3,2,1,0:T(8,128)S(1)} %fusion.121, f32[2,64,1024]{2,1,0:T(8,128)S(1)} %get-tuple-element.904, f32[2,64,1024]{2,1,0:T(8,128)S(1)} %get-tuple-element.927, f32[64,1024]{1,0:T(8,128)S(1)} %copy-done.12, ...), kind=kOutput, calls=%fused_computation.39.clone.1 | convolution fusion | flops 808452096 | bytes 2633984 | tf_op jit(solution)/shard_map/while/body/eval_jaxpr/szr,srx->szx/dot_general | solution.py:81
  206.1 4.9 %collective-permute-start.1 = (f32[4,2,8,1024]{3,2,1,0:T(8,128)}, f32[4,2,8,1024]{3,2,1,0:T(8,128)S(1)}, u32[]{:S(2)}, u32[]{:S(2)}) collective-permute-start(f32[4,2,8,1024]{3,2,1,0:T(8,128)} %get-tuple-element.863), channel_id=1, source_target_pairs={{0,1},{1,2},{2,3},{4,5},{5,6},{6,7},{8,9},{9,10},{10,11},{12,13},{... | collective-permute-start | bytes 786440 | tf_op jit(solution)/shard_map/while/body/eval_jaxpr/ppermute | solution.py:19
  213.6 1.6 collective-permute-done.1
  215.5 2.6 fusion.117
  219.1 3.2 %fusion.118 = f32[2,72,1024]{2,1,0:T(8,128)S(1)} fusion(f32[2,2,72,1024]{3,2,1,0:T(8,128)S(1)} %fusion.117, f32[4,2,80,1024]{3,2,1,0:T(8,128)S(1)} %pad_maximum_fusion.23, s32[2,512]{1,0:T(2,128)S(1)} %copy-done.17, f32[72,1024]{1,0:T(8,128)S(1)} %bitcast.101, f32[72,1024]{1,0:T(8,128)S(1)} %bitcast.98, f32[2,512]{1,0:T(2,128)S(1)} %get-tuple-element.864, ...), kind=kOutput, calls=%fused_computation.109.clone.1 | convolution fusion | flops 909246464 | bytes 2961696 | tf_op jit(solution)/shard_map/while/body/eval_jaxpr/szr,srx->szx/dot_general | solution.py:81
  222.4 2.4 fusion.121
  226.1 3.1 %fusion.122 = f32[2,64,1024]{2,1,0:T(8,128)S(1)} fusion(s32[2,512]{1,0:T(2,128)S(1)} %copy-done.17, f32[2,2,64,1024]{3,2,1,0:T(8,128)S(1)} %fusion.121, f32[2,64,1024]{2,1,0:T(8,128)S(1)} %get-tuple-element.904, f32[2,64,1024]{2,1,0:T(8,128)S(1)} %get-tuple-element.927, f32[64,1024]{1,0:T(8,128)S(1)} %copy-done.12, ...), kind=kOutput, calls=%fused_computation.39.clone.1 | convolution fusion | flops 808452096 | bytes 2633984 | tf_op jit(solution)/shard_map/while/body/eval_jaxpr/szr,srx->szx/dot_general | solution.py:81
  230.2 35.4 %all-reduce.4.cloned.1.call-done = f32[64,1024]{1,0:T(8,128)} async-done(((f32[64,1024]{1,0:T(8,128)}), f32[64,1024]{1,0:T(8,128)}) %all-reduce.4.cloned.1.call-update) | async-done | bytes 262160 | tf_op jit(solution)/shard_map/psum | solution.py:143
  265.6 1.7 broadcast_multiply_fusion
  (386 shorter events, 77.9 us)
Async XLA Ops:
  7.2 258.4 %all-reduce.4.cloned.1.call-start = ((), (), s32[]{:S(2)}) async-start(), calls=%async_computation | async-start | bytes 524288 | tf_op jit(solution)/shard_map/psum | solution.py:143
  7.2 1.7 copy-start.7
  7.2 8.2 %copy-start.13 = (f32[2,16,512]{2,1,0:T(8,128)S(1)}, f32[2,16,512]{2,1,0:T(8,128)}, u32[]{:S(2)}) copy-start(f32[2,16,512]{2,1,0:T(8,128)} %param.21) | copy-start | bytes 196612
  8.2 12.9 %copy-start.6 = (f32[2,64,1024]{2,1,0:T(8,128)S(1)}, f32[2,64,1024]{2,1,0:T(8,128)}, u32[]{:S(2)}) copy-start(f32[2,64,1024]{2,1,0:T(8,128)} %param.19) | copy-start | bytes 1572868
  8.9 12.1 %copy-start = (f32[256]{0:T(256)S(1)}, f32[256]{0:T(256)}, u32[]{:S(2)}) copy-start(f32[256]{0:T(256)} %param.22) | copy-start | bytes 3076
  8.9 12.1 %copy-start.1 = (f32[2,64,1024]{2,1,0:T(8,128)S(1)}, f32[2,64,1024]{2,1,0:T(8,128)}, u32[]{:S(2)}) copy-start(f32[2,64,1024]{2,1,0:T(8,128)} %param.17) | copy-start | bytes 1572868
  8.9 12.1 %copy-start.3 = (f32[2,64,1024]{2,1,0:T(8,128)S(1)}, f32[2,64,1024]{2,1,0:T(8,128)}, u32[]{:S(2)}) copy-start(f32[2,64,1024]{2,1,0:T(8,128)} %param.18) | copy-start | bytes 1572868
  8.9 12.1 %copy-start.5 = (f32[2,64,1024]{2,1,0:T(8,128)S(1)}, f32[2,64,1024]{2,1,0:T(8,128)}, u32[]{:S(2)}) copy-start(f32[2,64,1024]{2,1,0:T(8,128)} %param.20) | copy-start | bytes 1572868
  8.9 12.1 %copy-start.14 = (s32[2]{0:T(128)S(1)}, s32[2]{0:T(128)}, u32[]{:S(2)}) copy-start(s32[2]{0:T(128)} %param.27) | copy-start | bytes 28
  8.9 12.1 %copy-start.15 = (s32[2]{0:T(128)S(1)}, s32[2]{0:T(128)}, u32[]{:S(2)}) copy-start(s32[2]{0:T(128)} %param.24) | copy-start | bytes 28
  8.9 12.1 %copy-start.16 = (s32[2,512]{1,0:T(2,128)S(1)}, s32[2,512]{1,0:T(2,128)}, u32[]{:S(2)}) copy-start(s32[2,512]{1,0:T(2,128)} %param.25) | copy-start | bytes 12292
  9.0 12.1 %copy-start.18 = (s32[2]{0:T(128)S(1)}, s32[2]{0:T(128)}, u32[]{:S(2)}) copy-start(s32[2]{0:T(128)} %param.23) | copy-start | bytes 28
  9.0 7.0 %collective-permute-start.2 = (f32[2,8,1024]{2,1,0:T(8,128)S(1)}, f32[2,8,1024]{2,1,0:T(8,128)S(1)}, u32[]{:S(2)}, u32[]{:S(2)}) collective-permute-start(f32[2,8,1024]{2,1,0:T(8,128)S(1)} %get-tuple-element.729), channel_id=1, source_target_pairs={{0,1},{1,2},{2,3},{4,5},{5,6},{6,7},{8,9},{9,10},{10,11},{12,13},{... | collective-permute-start | bytes 196616 | tf_op jit(solution)/shard_map/ppermute | solution.py:19
  14.1 6.2 %collective-permute-start.3 = (f32[2,8,1024]{2,1,0:T(8,128)S(1)}, f32[2,8,1024]{2,1,0:T(8,128)S(1)}, u32[]{:S(2)}, u32[]{:S(2)}) collective-permute-start(f32[2,8,1024]{2,1,0:T(8,128)S(1)} %get-tuple-element.730), channel_id=1, source_target_pairs={{1,0},{2,1},{3,2},{5,4},{6,5},{7,6},{9,8},{10,9},{11,10},{13,12},{... | collective-permute-start | bytes 196616 | tf_op jit(solution)/shard_map/ppermute | solution.py:21
  21.9 8.7 %collective-permute-start = (f32[4,2,8,1024]{3,2,1,0:T(8,128)}, f32[4,2,8,1024]{3,2,1,0:T(8,128)S(1)}, u32[]{:S(2)}, u32[]{:S(2)}) collective-permute-start(f32[4,2,8,1024]{3,2,1,0:T(8,128)} %get-tuple-element.862), channel_id=1, source_target_pairs={{1,0},{2,1},{3,2},{5,4},{6,5},{7,6},{9,8},{10,9},{11,10},{13,12},{... | collective-permute-start | bytes 786440 | tf_op jit(solution)/shard_map/while/body/eval_jaxpr/ppermute | solution.py:21
  23.2 8.7 %collective-permute-start.1 = (f32[4,2,8,1024]{3,2,1,0:T(8,128)}, f32[4,2,8,1024]{3,2,1,0:T(8,128)S(1)}, u32[]{:S(2)}, u32[]{:S(2)}) collective-permute-start(f32[4,2,8,1024]{3,2,1,0:T(8,128)} %get-tuple-element.863), channel_id=1, source_target_pairs={{0,1},{1,2},{2,3},{4,5},{5,6},{6,7},{8,9},{9,10},{10,11},{12,13},{... | collective-permute-start | bytes 786440 | tf_op jit(solution)/shard_map/while/body/eval_jaxpr/ppermute | solution.py:19
  42.9 3.1 %copy-start.8 = (f32[64,1024]{1,0:T(8,128)S(1)}, f32[64,1024]{1,0:T(8,128)}, u32[]{:S(2)}) copy-start(f32[64,1024]{1,0:T(8,128)} %get-tuple-element.905) | copy-start | bytes 786436 | tf_op jit(solution)/shard_map/while
  42.9 4.0 %copy-start.19 = (s32[2]{0:T(128)S(1)}, s32[2]{0:T(128)}, u32[]{:S(2)}) copy-start(s32[2]{0:T(128)} %get-tuple-element.982) | copy-start | bytes 28 | tf_op jit(solution)/shard_map/while
  47.8 8.8 %collective-permute-start = (f32[4,2,8,1024]{3,2,1,0:T(8,128)}, f32[4,2,8,1024]{3,2,1,0:T(8,128)S(1)}, u32[]{:S(2)}, u32[]{:S(2)}) collective-permute-start(f32[4,2,8,1024]{3,2,1,0:T(8,128)} %get-tuple-element.862), channel_id=1, source_target_pairs={{1,0},{2,1},{3,2},{5,4},{6,5},{7,6},{9,8},{10,9},{11,10},{13,12},{... | collective-permute-start | bytes 786440 | tf_op jit(solution)/shard_map/while/body/eval_jaxpr/ppermute | solution.py:21
  49.0 9.1 %collective-permute-start.1 = (f32[4,2,8,1024]{3,2,1,0:T(8,128)}, f32[4,2,8,1024]{3,2,1,0:T(8,128)S(1)}, u32[]{:S(2)}, u32[]{:S(2)}) collective-permute-start(f32[4,2,8,1024]{3,2,1,0:T(8,128)} %get-tuple-element.863), channel_id=1, source_target_pairs={{0,1},{1,2},{2,3},{4,5},{5,6},{6,7},{8,9},{9,10},{10,11},{12,13},{... | collective-permute-start | bytes 786440 | tf_op jit(solution)/shard_map/while/body/eval_jaxpr/ppermute | solution.py:19
  69.1 3.1 %copy-start.8 = (f32[64,1024]{1,0:T(8,128)S(1)}, f32[64,1024]{1,0:T(8,128)}, u32[]{:S(2)}) copy-start(f32[64,1024]{1,0:T(8,128)} %get-tuple-element.905) | copy-start | bytes 786436 | tf_op jit(solution)/shard_map/while
  69.1 4.0 %copy-start.19 = (s32[2]{0:T(128)S(1)}, s32[2]{0:T(128)}, u32[]{:S(2)}) copy-start(s32[2]{0:T(128)} %get-tuple-element.982) | copy-start | bytes 28 | tf_op jit(solution)/shard_map/while
  73.9 8.8 %collective-permute-start = (f32[4,2,8,1024]{3,2,1,0:T(8,128)}, f32[4,2,8,1024]{3,2,1,0:T(8,128)S(1)}, u32[]{:S(2)}, u32[]{:S(2)}) collective-permute-start(f32[4,2,8,1024]{3,2,1,0:T(8,128)} %get-tuple-element.862), channel_id=1, source_target_pairs={{1,0},{2,1},{3,2},{5,4},{6,5},{7,6},{9,8},{10,9},{11,10},{13,12},{... | collective-permute-start | bytes 786440 | tf_op jit(solution)/shard_map/while/body/eval_jaxpr/ppermute | solution.py:21
  75.2 9.1 %collective-permute-start.1 = (f32[4,2,8,1024]{3,2,1,0:T(8,128)}, f32[4,2,8,1024]{3,2,1,0:T(8,128)S(1)}, u32[]{:S(2)}, u32[]{:S(2)}) collective-permute-start(f32[4,2,8,1024]{3,2,1,0:T(8,128)} %get-tuple-element.863), channel_id=1, source_target_pairs={{0,1},{1,2},{2,3},{4,5},{5,6},{6,7},{8,9},{9,10},{10,11},{12,13},{... | collective-permute-start | bytes 786440 | tf_op jit(solution)/shard_map/while/body/eval_jaxpr/ppermute | solution.py:19
  95.2 3.1 %copy-start.8 = (f32[64,1024]{1,0:T(8,128)S(1)}, f32[64,1024]{1,0:T(8,128)}, u32[]{:S(2)}) copy-start(f32[64,1024]{1,0:T(8,128)} %get-tuple-element.905) | copy-start | bytes 786436 | tf_op jit(solution)/shard_map/while
  95.2 4.0 %copy-start.19 = (s32[2]{0:T(128)S(1)}, s32[2]{0:T(128)}, u32[]{:S(2)}) copy-start(s32[2]{0:T(128)} %get-tuple-element.982) | copy-start | bytes 28 | tf_op jit(solution)/shard_map/while
  100.1 8.8 %collective-permute-start = (f32[4,2,8,1024]{3,2,1,0:T(8,128)}, f32[4,2,8,1024]{3,2,1,0:T(8,128)S(1)}, u32[]{:S(2)}, u32[]{:S(2)}) collective-permute-start(f32[4,2,8,1024]{3,2,1,0:T(8,128)} %get-tuple-element.862), channel_id=1, source_target_pairs={{1,0},{2,1},{3,2},{5,4},{6,5},{7,6},{9,8},{10,9},{11,10},{13,12},{... | collective-permute-start | bytes 786440 | tf_op jit(solution)/shard_map/while/body/eval_jaxpr/ppermute | solution.py:21
  101.4 9.1 %collective-permute-start.1 = (f32[4,2,8,1024]{3,2,1,0:T(8,128)}, f32[4,2,8,1024]{3,2,1,0:T(8,128)S(1)}, u32[]{:S(2)}, u32[]{:S(2)}) collective-permute-start(f32[4,2,8,1024]{3,2,1,0:T(8,128)} %get-tuple-element.863), channel_id=1, source_target_pairs={{0,1},{1,2},{2,3},{4,5},{5,6},{6,7},{8,9},{9,10},{10,11},{12,13},{... | collective-permute-start | bytes 786440 | tf_op jit(solution)/shard_map/while/body/eval_jaxpr/ppermute | solution.py:19
  121.4 3.1 %copy-start.8 = (f32[64,1024]{1,0:T(8,128)S(1)}, f32[64,1024]{1,0:T(8,128)}, u32[]{:S(2)}) copy-start(f32[64,1024]{1,0:T(8,128)} %get-tuple-element.905) | copy-start | bytes 786436 | tf_op jit(solution)/shard_map/while
  121.4 4.0 %copy-start.19 = (s32[2]{0:T(128)S(1)}, s32[2]{0:T(128)}, u32[]{:S(2)}) copy-start(s32[2]{0:T(128)} %get-tuple-element.982) | copy-start | bytes 28 | tf_op jit(solution)/shard_map/while
  126.3 8.8 %collective-permute-start = (f32[4,2,8,1024]{3,2,1,0:T(8,128)}, f32[4,2,8,1024]{3,2,1,0:T(8,128)S(1)}, u32[]{:S(2)}, u32[]{:S(2)}) collective-permute-start(f32[4,2,8,1024]{3,2,1,0:T(8,128)} %get-tuple-element.862), channel_id=1, source_target_pairs={{1,0},{2,1},{3,2},{5,4},{6,5},{7,6},{9,8},{10,9},{11,10},{13,12},{... | collective-permute-start | bytes 786440 | tf_op jit(solution)/shard_map/while/body/eval_jaxpr/ppermute | solution.py:21
  127.6 9.1 %collective-permute-start.1 = (f32[4,2,8,1024]{3,2,1,0:T(8,128)}, f32[4,2,8,1024]{3,2,1,0:T(8,128)S(1)}, u32[]{:S(2)}, u32[]{:S(2)}) collective-permute-start(f32[4,2,8,1024]{3,2,1,0:T(8,128)} %get-tuple-element.863), channel_id=1, source_target_pairs={{0,1},{1,2},{2,3},{4,5},{5,6},{6,7},{8,9},{9,10},{10,11},{12,13},{... | collective-permute-start | bytes 786440 | tf_op jit(solution)/shard_map/while/body/eval_jaxpr/ppermute | solution.py:19
  147.6 3.1 %copy-start.8 = (f32[64,1024]{1,0:T(8,128)S(1)}, f32[64,1024]{1,0:T(8,128)}, u32[]{:S(2)}) copy-start(f32[64,1024]{1,0:T(8,128)} %get-tuple-element.905) | copy-start | bytes 786436 | tf_op jit(solution)/shard_map/while
  147.6 4.0 %copy-start.19 = (s32[2]{0:T(128)S(1)}, s32[2]{0:T(128)}, u32[]{:S(2)}) copy-start(s32[2]{0:T(128)} %get-tuple-element.982) | copy-start | bytes 28 | tf_op jit(solution)/shard_map/while
  152.4 8.8 %collective-permute-start = (f32[4,2,8,1024]{3,2,1,0:T(8,128)}, f32[4,2,8,1024]{3,2,1,0:T(8,128)S(1)}, u32[]{:S(2)}, u32[]{:S(2)}) collective-permute-start(f32[4,2,8,1024]{3,2,1,0:T(8,128)} %get-tuple-element.862), channel_id=1, source_target_pairs={{1,0},{2,1},{3,2},{5,4},{6,5},{7,6},{9,8},{10,9},{11,10},{13,12},{... | collective-permute-start | bytes 786440 | tf_op jit(solution)/shard_map/while/body/eval_jaxpr/ppermute | solution.py:21
  153.7 9.1 %collective-permute-start.1 = (f32[4,2,8,1024]{3,2,1,0:T(8,128)}, f32[4,2,8,1024]{3,2,1,0:T(8,128)S(1)}, u32[]{:S(2)}, u32[]{:S(2)}) collective-permute-start(f32[4,2,8,1024]{3,2,1,0:T(8,128)} %get-tuple-element.863), channel_id=1, source_target_pairs={{0,1},{1,2},{2,3},{4,5},{5,6},{6,7},{8,9},{9,10},{10,11},{12,13},{... | collective-permute-start | bytes 786440 | tf_op jit(solution)/shard_map/while/body/eval_jaxpr/ppermute | solution.py:19
  173.8 3.1 %copy-start.8 = (f32[64,1024]{1,0:T(8,128)S(1)}, f32[64,1024]{1,0:T(8,128)}, u32[]{:S(2)}) copy-start(f32[64,1024]{1,0:T(8,128)} %get-tuple-element.905) | copy-start | bytes 786436 | tf_op jit(solution)/shard_map/while
  173.8 4.0 %copy-start.19 = (s32[2]{0:T(128)S(1)}, s32[2]{0:T(128)}, u32[]{:S(2)}) copy-start(s32[2]{0:T(128)} %get-tuple-element.982) | copy-start | bytes 28 | tf_op jit(solution)/shard_map/while
  178.6 8.8 %collective-permute-start = (f32[4,2,8,1024]{3,2,1,0:T(8,128)}, f32[4,2,8,1024]{3,2,1,0:T(8,128)S(1)}, u32[]{:S(2)}, u32[]{:S(2)}) collective-permute-start(f32[4,2,8,1024]{3,2,1,0:T(8,128)} %get-tuple-element.862), channel_id=1, source_target_pairs={{1,0},{2,1},{3,2},{5,4},{6,5},{7,6},{9,8},{10,9},{11,10},{13,12},{... | collective-permute-start | bytes 786440 | tf_op jit(solution)/shard_map/while/body/eval_jaxpr/ppermute | solution.py:21
  179.9 9.1 %collective-permute-start.1 = (f32[4,2,8,1024]{3,2,1,0:T(8,128)}, f32[4,2,8,1024]{3,2,1,0:T(8,128)S(1)}, u32[]{:S(2)}, u32[]{:S(2)}) collective-permute-start(f32[4,2,8,1024]{3,2,1,0:T(8,128)} %get-tuple-element.863), channel_id=1, source_target_pairs={{0,1},{1,2},{2,3},{4,5},{5,6},{6,7},{8,9},{9,10},{10,11},{12,13},{... | collective-permute-start | bytes 786440 | tf_op jit(solution)/shard_map/while/body/eval_jaxpr/ppermute | solution.py:19
  199.9 3.1 %copy-start.8 = (f32[64,1024]{1,0:T(8,128)S(1)}, f32[64,1024]{1,0:T(8,128)}, u32[]{:S(2)}) copy-start(f32[64,1024]{1,0:T(8,128)} %get-tuple-element.905) | copy-start | bytes 786436 | tf_op jit(solution)/shard_map/while
  199.9 4.0 %copy-start.19 = (s32[2]{0:T(128)S(1)}, s32[2]{0:T(128)}, u32[]{:S(2)}) copy-start(s32[2]{0:T(128)} %get-tuple-element.982) | copy-start | bytes 28 | tf_op jit(solution)/shard_map/while
  204.8 8.8 %collective-permute-start = (f32[4,2,8,1024]{3,2,1,0:T(8,128)}, f32[4,2,8,1024]{3,2,1,0:T(8,128)S(1)}, u32[]{:S(2)}, u32[]{:S(2)}) collective-permute-start(f32[4,2,8,1024]{3,2,1,0:T(8,128)} %get-tuple-element.862), channel_id=1, source_target_pairs={{1,0},{2,1},{3,2},{5,4},{6,5},{7,6},{9,8},{10,9},{11,10},{13,12},{... | collective-permute-start | bytes 786440 | tf_op jit(solution)/shard_map/while/body/eval_jaxpr/ppermute | solution.py:21
  206.1 9.1 %collective-permute-start.1 = (f32[4,2,8,1024]{3,2,1,0:T(8,128)}, f32[4,2,8,1024]{3,2,1,0:T(8,128)S(1)}, u32[]{:S(2)}, u32[]{:S(2)}) collective-permute-start(f32[4,2,8,1024]{3,2,1,0:T(8,128)} %get-tuple-element.863), channel_id=1, source_target_pairs={{0,1},{1,2},{2,3},{4,5},{5,6},{6,7},{8,9},{9,10},{10,11},{12,13},{... | collective-permute-start | bytes 786440 | tf_op jit(solution)/shard_map/while/body/eval_jaxpr/ppermute | solution.py:19
  226.1 3.1 %copy-start.8 = (f32[64,1024]{1,0:T(8,128)S(1)}, f32[64,1024]{1,0:T(8,128)}, u32[]{:S(2)}) copy-start(f32[64,1024]{1,0:T(8,128)} %get-tuple-element.905) | copy-start | bytes 786436 | tf_op jit(solution)/shard_map/while
  226.1 4.0 %copy-start.19 = (s32[2]{0:T(128)S(1)}, s32[2]{0:T(128)}, u32[]{:S(2)}) copy-start(s32[2]{0:T(128)} %get-tuple-element.982) | copy-start | bytes 28 | tf_op jit(solution)/shard_map/while
  230.1 37.1 %copy-start.2 = (f32[2,64,1024]{2,1,0:T(8,128)}, f32[2,64,1024]{2,1,0:T(8,128)S(1)}, u32[]{:S(2)}) copy-start(f32[2,64,1024]{2,1,0:T(8,128)S(1)} %get-tuple-element.960) | copy-start | bytes 1572868
  230.1 37.1 %copy-start.4 = (f32[2,64,1024]{2,1,0:T(8,128)}, f32[2,64,1024]{2,1,0:T(8,128)S(1)}, u32[]{:S(2)}) copy-start(f32[2,64,1024]{2,1,0:T(8,128)S(1)} %get-tuple-element.962) | copy-start | bytes 1572868
  (65 other events, 53.8 us)
Sparse Core Ops, SparseCore 0:
  230.3 35.2 all-reduce.3
where the time goes:
time: 275 us; the launch traced here: 274 us
  other arithmetic  63.9 us (23%)
  waiting for transfers between devices  56.8 us (21%)
  starting transfers between devices  55.7 us (20%)
  matrix products  50.3 us (18%)
  local copies, waits for them, and re-layouts  31.5 us (11%)
  between operations  14.2 us (5%)
    dot_general x16, matrix products, advance(): jnp.einsum('szr,srx->szx', depth_table, lateral_table, precision=lax.Prec...  50.3 us
    ppermute x9, starting transfers between devices, extended_2(): lax.ppermute(tail, axis, [(i, (i + 1) % count) for i in range(ends)])  44.1 us
    add x16, other arithmetic, laplace(): result + stencil_coeffs[offset] * (extended[..., 4 + offset:4 + offset +...  39.8 us
    psum x1, waiting for transfers between devices, local(): image_total = lax.psum(carry[4], 'shot')  35.4 us
    while x160, local copies, waits for them, and re-layouts  18.2 us
    ppermute x9, waiting for transfers between devices, extended_2(): lax.ppermute(tail, axis, [(i, (i + 1) % count) for i in range(ends)])  12.8 us
    ppermute x9, starting transfers between devices, extended_2(): lax.ppermute(head, axis, [((i + 1) % count, i) for i in range(ends)])  11.5 us
    gather x16, local copies, waits for them, and re-layouts, advance(): pulse = wavelet[checkpoint_step + STEPS - 1 - step_index]  10.2 us
  transfers between devices with their start and end apart: 19, of which 19 were waited for; matrix products, arithmetic and copies ran while one was open for 5% of the time, Pallas kernels for 0%

commit v1 on v0

--- a/solution.py
+++ b/solution.py
@@ -140,7 +140,9 @@
     )
     source_final = carry[1]
     receiver_final = carry[3]
-    image_total = lax.psum(carry[4], "shot")
+    block = carry[4]
+    pieces = lax.all_gather(block, "shot")
+    image_total = jnp.sum(pieces, axis=0)
     shots_all = lax.axis_size("shot") * source_now.shape[0]
     image = image_total / math.sqrt(STEPS * shots_all)
     return (image, source_final, receiver_final)

time: 275 us -> 260 us (0.945)
  waiting for transfers between devices: 56.8 us -> 41.2 us
    psum x1 -> x0, waiting for transfers between devices: 35.4 us -> none  [local(): image_total = lax.psum(carry[4], 'shot')]
    all_gather x0 -> x1, waiting for transfers between devices: none -> 19.8 us  [local(): pieces = lax.all_gather(block, 'shot')]
where the time goes in v1:
time: 260 us; the launch traced here: 259 us
  other arithmetic  64.2 us (25%)
  starting transfers between devices  55.7 us (21%)
  matrix products  50.3 us (19%)
  waiting for transfers between devices  41.2 us (16%)
  local copies, waits for them, and re-layouts  31.5 us (12%)
  between operations  14.2 us (5%)
    dot_general x16, matrix products, advance(): jnp.einsum('szr,srx->szx', depth_table, lateral_table, precision=lax.Prec...  50.3 us
    ppermute x9, starting transfers between devices, extended_2(): lax.ppermute(tail, axis, [(i, (i + 1) % count) for i in range(ends)])  44.1 us
    add x16, other arithmetic, laplace(): result + stencil_coeffs[offset] * (extended[..., 4 + offset:4 + offset +...  39.8 us
    all_gather x1, waiting for transfers between devices, local(): pieces = lax.all_gather(block, 'shot')  19.8 us
    while x160, local copies, waits for them, and re-layouts  18.2 us
    ppermute x9, waiting for transfers between devices, extended_2(): lax.ppermute(tail, axis, [(i, (i + 1) % count) for i in range(ends)])  12.8 us
    ppermute x9, starting transfers between devices, extended_2(): lax.ppermute(head, axis, [((i + 1) % count, i) for i in range(ends)])  11.5 us
    gather x16, local copies, waits for them, and re-layouts, advance(): pulse = wavelet[checkpoint_step + STEPS - 1 - step_index]  10.2 us
  transfers between devices with their start and end apart: 19, of which 19 were waited for; matrix products, arithmetic and copies ran while one was open for 5% of the time, Pallas kernels for 0%

profile of v1, /device:TPU:0, one launch (start us, length us, event | category | flops | bytes accessed | tf_op | source)
XLA Modules:
  0.0 258.9 jit_solution(11794666047563097001)
XLA Ops:
  9.0 5.1 %collective-permute-start.2 = (f32[2,8,1024]{2,1,0:T(8,128)S(1)}, f32[2,8,1024]{2,1,0:T(8,128)S(1)}, u32[]{:S(2)}, u32[]{:S(2)}) collective-permute-start(f32[2,8,1024]{2,1,0:T(8,128)S(1)} %get-tuple-element.729), channel_id=1, source_target_pairs={{0,1},{1,2},{2,3},{4,5},{5,6},{6,7},{8,9},{9,10},{10,11},{12,13},{... | collective-permute-start | bytes 196616 | tf_op jit(solution)/shard_map/ppermute | solution.py:19
  16.0 4.3 %collective-permute-done.3 = f32[2,8,1024]{2,1,0:T(8,128)S(1)} collective-permute-done((f32[2,8,1024]{2,1,0:T(8,128)S(1)}, f32[2,8,1024]{2,1,0:T(8,128)S(1)}, u32[]{:S(2)}, u32[]{:S(2)}) %collective-permute-start.3) | collective-permute-done | bytes 65568 | tf_op jit(solution)/shard_map/ppermute | solution.py:21
  21.1 209.0 %while.26 = (s32[]{:T(128)}, f32[2,64,1024]{2,1,0:T(8,128)S(1)}, f32[2,64,1024]{2,1,0:T(8,128)S(1)}, f32[2,64,1024]{2,1,0:T(8,128)S(1)}, f32[2,64,1024]{2,1,0:T(...) while((s32[]{:T(128)}, f32[2,64,1024]{2,1,0:T(8,128)S(1)}, ...), condition=%wide.region_3.4_spmd.clone, body=%wide.region_0.3_spmd.clone.sunk | while | flops 1741394304 | bytes 51560036 | solution.py:135
  23.2 4.6 %collective-permute-start.1 = (f32[4,2,8,1024]{3,2,1,0:T(8,128)}, f32[4,2,8,1024]{3,2,1,0:T(8,128)S(1)}, u32[]{:S(2)}, u32[]{:S(2)}) collective-permute-start(f32[4,2,8,1024]{3,2,1,0:T(8,128)} %get-tuple-element.863), channel_id=1, source_target_pairs={{0,1},{1,2},{2,3},{4,5},{5,6},{6,7},{8,9},{9,10},{10,11},{12,13},{... | collective-permute-start | bytes 786440 | tf_op jit(solution)/shard_map/while/body/eval_jaxpr/ppermute | solution.py:19
  32.3 2.6 %fusion.117 = f32[2,2,72,1024]{3,2,1,0:T(8,128)S(1)} fusion(f32[2,2,72,1024]{3,2,1,0:T(8,128)S(1)} %slice.1057, f32[4,2,8,1024]{3,2,1,0:T(8,128)S(1)} %collective-permute-done.1, f32[1,2,64,1024]{3,2,1,0:T(8,128)S(1)} %bitcast.94, f32[1,2,64,1024]{3,2,1,0:T(8,128)S(1)} %bitcast.85, f32[1,2,64,1024]{3,2,1,0:T(8,128)S(1)} %bitcast.91, ...), kind=kLoop, calls=%fused_computation.46.clone.1 | loop fusion | flops 8552448 | bytes 12058624 | tf_op jit(solution)/shard_map/while/body/eval_jaxpr/add | solution.py:36
  35.9 3.2 %fusion.118 = f32[2,72,1024]{2,1,0:T(8,128)S(1)} fusion(f32[2,2,72,1024]{3,2,1,0:T(8,128)S(1)} %fusion.117, f32[4,2,80,1024]{3,2,1,0:T(8,128)S(1)} %pad_maximum_fusion.23, s32[2,512]{1,0:T(2,128)S(1)} %copy-done.17, f32[72,1024]{1,0:T(8,128)S(1)} %bitcast.103, f32[72,1024]{1,0:T(8,128)S(1)} %bitcast.99, f32[2,512]{1,0:T(2,128)S(1)} %get-tuple-element.864, ...), kind=kOutput, calls=%fused_computation.109.clone.1 | convolution fusion | flops 909246464 | bytes 2961696 | tf_op jit(solution)/shard_map/while/body/eval_jaxpr/szr,srx->szx/dot_general | solution.py:81
  39.2 2.4 fusion.121
  42.9 3.1 %fusion.122 = f32[2,64,1024]{2,1,0:T(8,128)S(1)} fusion(s32[2,512]{1,0:T(2,128)S(1)} %copy-done.17, f32[2,2,64,1024]{3,2,1,0:T(8,128)S(1)} %fusion.121, f32[2,64,1024]{2,1,0:T(8,128)S(1)} %get-tuple-element.904, f32[2,64,1024]{2,1,0:T(8,128)S(1)} %get-tuple-element.927, f32[64,1024]{1,0:T(8,128)S(1)} %copy-done.12, ...), kind=kOutput, calls=%fused_computation.39.clone.1 | convolution fusion | flops 808452096 | bytes 2633984 | tf_op jit(solution)/shard_map/while/body/eval_jaxpr/szr,srx->szx/dot_general | solution.py:81
  49.0 4.9 %collective-permute-start.1 = (f32[4,2,8,1024]{3,2,1,0:T(8,128)}, f32[4,2,8,1024]{3,2,1,0:T(8,128)S(1)}, u32[]{:S(2)}, u32[]{:S(2)}) collective-permute-start(f32[4,2,8,1024]{3,2,1,0:T(8,128)} %get-tuple-element.863), channel_id=1, source_target_pairs={{0,1},{1,2},{2,3},{4,5},{5,6},{6,7},{8,9},{9,10},{10,11},{12,13},{... | collective-permute-start | bytes 786440 | tf_op jit(solution)/shard_map/while/body/eval_jaxpr/ppermute | solution.py:19
  56.6 1.6 collective-permute-done.1
  58.5 2.6 %fusion.117 = f32[2,2,72,1024]{3,2,1,0:T(8,128)S(1)} fusion(f32[2,2,72,1024]{3,2,1,0:T(8,128)S(1)} %slice.1057, f32[4,2,8,1024]{3,2,1,0:T(8,128)S(1)} %collective-permute-done.1, f32[1,2,64,1024]{3,2,1,0:T(8,128)S(1)} %bitcast.94, f32[1,2,64,1024]{3,2,1,0:T(8,128)S(1)} %bitcast.85, f32[1,2,64,1024]{3,2,1,0:T(8,128)S(1)} %bitcast.91, ...), kind=kLoop, calls=%fused_computation.46.clone.1 | loop fusion | flops 8552448 | bytes 12058624 | tf_op jit(solution)/shard_map/while/body/eval_jaxpr/add | solution.py:36
  62.1 3.2 %fusion.118 = f32[2,72,1024]{2,1,0:T(8,128)S(1)} fusion(f32[2,2,72,1024]{3,2,1,0:T(8,128)S(1)} %fusion.117, f32[4,2,80,1024]{3,2,1,0:T(8,128)S(1)} %pad_maximum_fusion.23, s32[2,512]{1,0:T(2,128)S(1)} %copy-done.17, f32[72,1024]{1,0:T(8,128)S(1)} %bitcast.103, f32[72,1024]{1,0:T(8,128)S(1)} %bitcast.99, f32[2,512]{1,0:T(2,128)S(1)} %get-tuple-element.864, ...), kind=kOutput, calls=%fused_computation.109.clone.1 | convolution fusion | flops 909246464 | bytes 2961696 | tf_op jit(solution)/shard_map/while/body/eval_jaxpr/szr,srx->szx/dot_general | solution.py:81
  65.4 2.4 fusion.121
  69.1 3.1 %fusion.122 = f32[2,64,1024]{2,1,0:T(8,128)S(1)} fusion(s32[2,512]{1,0:T(2,128)S(1)} %copy-done.17, f32[2,2,64,1024]{3,2,1,0:T(8,128)S(1)} %fusion.121, f32[2,64,1024]{2,1,0:T(8,128)S(1)} %get-tuple-element.904, f32[2,64,1024]{2,1,0:T(8,128)S(1)} %get-tuple-element.927, f32[64,1024]{1,0:T(8,128)S(1)} %copy-done.12, ...), kind=kOutput, calls=%fused_computation.39.clone.1 | convolution fusion | flops 808452096 | bytes 2633984 | tf_op jit(solution)/shard_map/while/body/eval_jaxpr/szr,srx->szx/dot_general | solution.py:81
  75.2 4.9 %collective-permute-start.1 = (f32[4,2,8,1024]{3,2,1,0:T(8,128)}, f32[4,2,8,1024]{3,2,1,0:T(8,128)S(1)}, u32[]{:S(2)}, u32[]{:S(2)}) collective-permute-start(f32[4,2,8,1024]{3,2,1,0:T(8,128)} %get-tuple-element.863), channel_id=1, source_target_pairs={{0,1},{1,2},{2,3},{4,5},{5,6},{6,7},{8,9},{9,10},{10,11},{12,13},{... | collective-permute-start | bytes 786440 | tf_op jit(solution)/shard_map/while/body/eval_jaxpr/ppermute | solution.py:19
  82.8 1.6 collective-permute-done.1
  84.7 2.6 %fusion.117 = f32[2,2,72,1024]{3,2,1,0:T(8,128)S(1)} fusion(f32[2,2,72,1024]{3,2,1,0:T(8,128)S(1)} %slice.1057, f32[4,2,8,1024]{3,2,1,0:T(8,128)S(1)} %collective-permute-done.1, f32[1,2,64,1024]{3,2,1,0:T(8,128)S(1)} %bitcast.94, f32[1,2,64,1024]{3,2,1,0:T(8,128)S(1)} %bitcast.85, f32[1,2,64,1024]{3,2,1,0:T(8,128)S(1)} %bitcast.91, ...), kind=kLoop, calls=%fused_computation.46.clone.1 | loop fusion | flops 8552448 | bytes 12058624 | tf_op jit(solution)/shard_map/while/body/eval_jaxpr/add | solution.py:36
  88.3 3.2 %fusion.118 = f32[2,72,1024]{2,1,0:T(8,128)S(1)} fusion(f32[2,2,72,1024]{3,2,1,0:T(8,128)S(1)} %fusion.117, f32[4,2,80,1024]{3,2,1,0:T(8,128)S(1)} %pad_maximum_fusion.23, s32[2,512]{1,0:T(2,128)S(1)} %copy-done.17, f32[72,1024]{1,0:T(8,128)S(1)} %bitcast.103, f32[72,1024]{1,0:T(8,128)S(1)} %bitcast.99, f32[2,512]{1,0:T(2,128)S(1)} %get-tuple-element.864, ...), kind=kOutput, calls=%fused_computation.109.clone.1 | convolution fusion | flops 909246464 | bytes 2961696 | tf_op jit(solution)/shard_map/while/body/eval_jaxpr/szr,srx->szx/dot_general | solution.py:81
  91.6 2.4 fusion.121
  95.2 3.1 %fusion.122 = f32[2,64,1024]{2,1,0:T(8,128)S(1)} fusion(s32[2,512]{1,0:T(2,128)S(1)} %copy-done.17, f32[2,2,64,1024]{3,2,1,0:T(8,128)S(1)} %fusion.121, f32[2,64,1024]{2,1,0:T(8,128)S(1)} %get-tuple-element.904, f32[2,64,1024]{2,1,0:T(8,128)S(1)} %get-tuple-element.927, f32[64,1024]{1,0:T(8,128)S(1)} %copy-done.12, ...), kind=kOutput, calls=%fused_computation.39.clone.1 | convolution fusion | flops 808452096 | bytes 2633984 | tf_op jit(solution)/shard_map/while/body/eval_jaxpr/szr,srx->szx/dot_general | solution.py:81
  101.4 4.9 %collective-permute-start.1 = (f32[4,2,8,1024]{3,2,1,0:T(8,128)}, f32[4,2,8,1024]{3,2,1,0:T(8,128)S(1)}, u32[]{:S(2)}, u32[]{:S(2)}) collective-permute-start(f32[4,2,8,1024]{3,2,1,0:T(8,128)} %get-tuple-element.863), channel_id=1, source_target_pairs={{0,1},{1,2},{2,3},{4,5},{5,6},{6,7},{8,9},{9,10},{10,11},{12,13},{... | collective-permute-start | bytes 786440 | tf_op jit(solution)/shard_map/while/body/eval_jaxpr/ppermute | solution.py:19
  108.9 1.6 collective-permute-done.1
  110.8 2.6 %fusion.117 = f32[2,2,72,1024]{3,2,1,0:T(8,128)S(1)} fusion(f32[2,2,72,1024]{3,2,1,0:T(8,128)S(1)} %slice.1057, f32[4,2,8,1024]{3,2,1,0:T(8,128)S(1)} %collective-permute-done.1, f32[1,2,64,1024]{3,2,1,0:T(8,128)S(1)} %bitcast.94, f32[1,2,64,1024]{3,2,1,0:T(8,128)S(1)} %bitcast.85, f32[1,2,64,1024]{3,2,1,0:T(8,128)S(1)} %bitcast.91, ...), kind=kLoop, calls=%fused_computation.46.clone.1 | loop fusion | flops 8552448 | bytes 12058624 | tf_op jit(solution)/shard_map/while/body/eval_jaxpr/add | solution.py:36
  114.4 3.2 %fusion.118 = f32[2,72,1024]{2,1,0:T(8,128)S(1)} fusion(f32[2,2,72,1024]{3,2,1,0:T(8,128)S(1)} %fusion.117, f32[4,2,80,1024]{3,2,1,0:T(8,128)S(1)} %pad_maximum_fusion.23, s32[2,512]{1,0:T(2,128)S(1)} %copy-done.17, f32[72,1024]{1,0:T(8,128)S(1)} %bitcast.103, f32[72,1024]{1,0:T(8,128)S(1)} %bitcast.99, f32[2,512]{1,0:T(2,128)S(1)} %get-tuple-element.864, ...), kind=kOutput, calls=%fused_computation.109.clone.1 | convolution fusion | flops 909246464 | bytes 2961696 | tf_op jit(solution)/shard_map/while/body/eval_jaxpr/szr,srx->szx/dot_general | solution.py:81
  117.8 2.4 fusion.121
  121.4 3.1 %fusion.122 = f32[2,64,1024]{2,1,0:T(8,128)S(1)} fusion(s32[2,512]{1,0:T(2,128)S(1)} %copy-done.17, f32[2,2,64,1024]{3,2,1,0:T(8,128)S(1)} %fusion.121, f32[2,64,1024]{2,1,0:T(8,128)S(1)} %get-tuple-element.904, f32[2,64,1024]{2,1,0:T(8,128)S(1)} %get-tuple-element.927, f32[64,1024]{1,0:T(8,128)S(1)} %copy-done.12, ...), kind=kOutput, calls=%fused_computation.39.clone.1 | convolution fusion | flops 808452096 | bytes 2633984 | tf_op jit(solution)/shard_map/while/body/eval_jaxpr/szr,srx->szx/dot_general | solution.py:81
  127.6 4.9 %collective-permute-start.1 = (f32[4,2,8,1024]{3,2,1,0:T(8,128)}, f32[4,2,8,1024]{3,2,1,0:T(8,128)S(1)}, u32[]{:S(2)}, u32[]{:S(2)}) collective-permute-start(f32[4,2,8,1024]{3,2,1,0:T(8,128)} %get-tuple-element.863), channel_id=1, source_target_pairs={{0,1},{1,2},{2,3},{4,5},{5,6},{6,7},{8,9},{9,10},{10,11},{12,13},{... | collective-permute-start | bytes 786440 | tf_op jit(solution)/shard_map/while/body/eval_jaxpr/ppermute | solution.py:19
  137.0 2.6 %fusion.117 = f32[2,2,72,1024]{3,2,1,0:T(8,128)S(1)} fusion(f32[2,2,72,1024]{3,2,1,0:T(8,128)S(1)} %slice.1057, f32[4,2,8,1024]{3,2,1,0:T(8,128)S(1)} %collective-permute-done.1, f32[1,2,64,1024]{3,2,1,0:T(8,128)S(1)} %bitcast.94, f32[1,2,64,1024]{3,2,1,0:T(8,128)S(1)} %bitcast.85, f32[1,2,64,1024]{3,2,1,0:T(8,128)S(1)} %bitcast.91, ...), kind=kLoop, calls=%fused_computation.46.clone.1 | loop fusion | flops 8552448 | bytes 12058624 | tf_op jit(solution)/shard_map/while/body/eval_jaxpr/add | solution.py:36
  140.6 3.2 %fusion.118 = f32[2,72,1024]{2,1,0:T(8,128)S(1)} fusion(f32[2,2,72,1024]{3,2,1,0:T(8,128)S(1)} %fusion.117, f32[4,2,80,1024]{3,2,1,0:T(8,128)S(1)} %pad_maximum_fusion.23, s32[2,512]{1,0:T(2,128)S(1)} %copy-done.17, f32[72,1024]{1,0:T(8,128)S(1)} %bitcast.103, f32[72,1024]{1,0:T(8,128)S(1)} %bitcast.99, f32[2,512]{1,0:T(2,128)S(1)} %get-tuple-element.864, ...), kind=kOutput, calls=%fused_computation.109.clone.1 | convolution fusion | flops 909246464 | bytes 2961696 | tf_op jit(solution)/shard_map/while/body/eval_jaxpr/szr,srx->szx/dot_general | solution.py:81
  143.9 2.4 fusion.121
  147.6 3.1 %fusion.122 = f32[2,64,1024]{2,1,0:T(8,128)S(1)} fusion(s32[2,512]{1,0:T(2,128)S(1)} %copy-done.17, f32[2,2,64,1024]{3,2,1,0:T(8,128)S(1)} %fusion.121, f32[2,64,1024]{2,1,0:T(8,128)S(1)} %get-tuple-element.904, f32[2,64,1024]{2,1,0:T(8,128)S(1)} %get-tuple-element.927, f32[64,1024]{1,0:T(8,128)S(1)} %copy-done.12, ...), kind=kOutput, calls=%fused_computation.39.clone.1 | convolution fusion | flops 808452096 | bytes 2633984 | tf_op jit(solution)/shard_map/while/body/eval_jaxpr/szr,srx->szx/dot_general | solution.py:81
  153.7 4.9 %collective-permute-start.1 = (f32[4,2,8,1024]{3,2,1,0:T(8,128)}, f32[4,2,8,1024]{3,2,1,0:T(8,128)S(1)}, u32[]{:S(2)}, u32[]{:S(2)}) collective-permute-start(f32[4,2,8,1024]{3,2,1,0:T(8,128)} %get-tuple-element.863), channel_id=1, source_target_pairs={{0,1},{1,2},{2,3},{4,5},{5,6},{6,7},{8,9},{9,10},{10,11},{12,13},{... | collective-permute-start | bytes 786440 | tf_op jit(solution)/shard_map/while/body/eval_jaxpr/ppermute | solution.py:19
  163.2 2.6 %fusion.117 = f32[2,2,72,1024]{3,2,1,0:T(8,128)S(1)} fusion(f32[2,2,72,1024]{3,2,1,0:T(8,128)S(1)} %slice.1057, f32[4,2,8,1024]{3,2,1,0:T(8,128)S(1)} %collective-permute-done.1, f32[1,2,64,1024]{3,2,1,0:T(8,128)S(1)} %bitcast.94, f32[1,2,64,1024]{3,2,1,0:T(8,128)S(1)} %bitcast.85, f32[1,2,64,1024]{3,2,1,0:T(8,128)S(1)} %bitcast.91, ...), kind=kLoop, calls=%fused_computation.46.clone.1 | loop fusion | flops 8552448 | bytes 12058624 | tf_op jit(solution)/shard_map/while/body/eval_jaxpr/add | solution.py:36
  166.8 3.2 %fusion.118 = f32[2,72,1024]{2,1,0:T(8,128)S(1)} fusion(f32[2,2,72,1024]{3,2,1,0:T(8,128)S(1)} %fusion.117, f32[4,2,80,1024]{3,2,1,0:T(8,128)S(1)} %pad_maximum_fusion.23, s32[2,512]{1,0:T(2,128)S(1)} %copy-done.17, f32[72,1024]{1,0:T(8,128)S(1)} %bitcast.103, f32[72,1024]{1,0:T(8,128)S(1)} %bitcast.99, f32[2,512]{1,0:T(2,128)S(1)} %get-tuple-element.864, ...), kind=kOutput, calls=%fused_computation.109.clone.1 | convolution fusion | flops 909246464 | bytes 2961696 | tf_op jit(solution)/shard_map/while/body/eval_jaxpr/szr,srx->szx/dot_general | solution.py:81
  170.1 2.4 fusion.121
  173.8 3.1 %fusion.122 = f32[2,64,1024]{2,1,0:T(8,128)S(1)} fusion(s32[2,512]{1,0:T(2,128)S(1)} %copy-done.17, f32[2,2,64,1024]{3,2,1,0:T(8,128)S(1)} %fusion.121, f32[2,64,1024]{2,1,0:T(8,128)S(1)} %get-tuple-element.904, f32[2,64,1024]{2,1,0:T(8,128)S(1)} %get-tuple-element.927, f32[64,1024]{1,0:T(8,128)S(1)} %copy-done.12, ...), kind=kOutput, calls=%fused_computation.39.clone.1 | convolution fusion | flops 808452096 | bytes 2633984 | tf_op jit(solution)/shard_map/while/body/eval_jaxpr/szr,srx->szx/dot_general | solution.py:81
  179.9 4.9 %collective-permute-start.1 = (f32[4,2,8,1024]{3,2,1,0:T(8,128)}, f32[4,2,8,1024]{3,2,1,0:T(8,128)S(1)}, u32[]{:S(2)}, u32[]{:S(2)}) collective-permute-start(f32[4,2,8,1024]{3,2,1,0:T(8,128)} %get-tuple-element.863), channel_id=1, source_target_pairs={{0,1},{1,2},{2,3},{4,5},{5,6},{6,7},{8,9},{9,10},{10,11},{12,13},{... | collective-permute-start | bytes 786440 | tf_op jit(solution)/shard_map/while/body/eval_jaxpr/ppermute | solution.py:19
  189.4 2.6 %fusion.117 = f32[2,2,72,1024]{3,2,1,0:T(8,128)S(1)} fusion(f32[2,2,72,1024]{3,2,1,0:T(8,128)S(1)} %slice.1057, f32[4,2,8,1024]{3,2,1,0:T(8,128)S(1)} %collective-permute-done.1, f32[1,2,64,1024]{3,2,1,0:T(8,128)S(1)} %bitcast.94, f32[1,2,64,1024]{3,2,1,0:T(8,128)S(1)} %bitcast.85, f32[1,2,64,1024]{3,2,1,0:T(8,128)S(1)} %bitcast.91, ...), kind=kLoop, calls=%fused_computation.46.clone.1 | loop fusion | flops 8552448 | bytes 12058624 | tf_op jit(solution)/shard_map/while/body/eval_jaxpr/add | solution.py:36
  193.0 3.2 %fusion.118 = f32[2,72,1024]{2,1,0:T(8,128)S(1)} fusion(f32[2,2,72,1024]{3,2,1,0:T(8,128)S(1)} %fusion.117, f32[4,2,80,1024]{3,2,1,0:T(8,128)S(1)} %pad_maximum_fusion.23, s32[2,512]{1,0:T(2,128)S(1)} %copy-done.17, f32[72,1024]{1,0:T(8,128)S(1)} %bitcast.103, f32[72,1024]{1,0:T(8,128)S(1)} %bitcast.99, f32[2,512]{1,0:T(2,128)S(1)} %get-tuple-element.864, ...), kind=kOutput, calls=%fused_computation.109.clone.1 | convolution fusion | flops 909246464 | bytes 2961696 | tf_op jit(solution)/shard_map/while/body/eval_jaxpr/szr,srx->szx/dot_general | solution.py:81
  196.3 2.4 fusion.121
  199.9 3.1 %fusion.122 = f32[2,64,1024]{2,1,0:T(8,128)S(1)} fusion(s32[2,512]{1,0:T(2,128)S(1)} %copy-done.17, f32[2,2,64,1024]{3,2,1,0:T(8,128)S(1)} %fusion.121, f32[2,64,1024]{2,1,0:T(8,128)S(1)} %get-tuple-element.904, f32[2,64,1024]{2,1,0:T(8,128)S(1)} %get-tuple-element.927, f32[64,1024]{1,0:T(8,128)S(1)} %copy-done.12, ...), kind=kOutput, calls=%fused_computation.39.clone.1 | convolution fusion | flops 808452096 | bytes 2633984 | tf_op jit(solution)/shard_map/while/body/eval_jaxpr/szr,srx->szx/dot_general | solution.py:81
  206.1 4.9 %collective-permute-start.1 = (f32[4,2,8,1024]{3,2,1,0:T(8,128)}, f32[4,2,8,1024]{3,2,1,0:T(8,128)S(1)}, u32[]{:S(2)}, u32[]{:S(2)}) collective-permute-start(f32[4,2,8,1024]{3,2,1,0:T(8,128)} %get-tuple-element.863), channel_id=1, source_target_pairs={{0,1},{1,2},{2,3},{4,5},{5,6},{6,7},{8,9},{9,10},{10,11},{12,13},{... | collective-permute-start | bytes 786440 | tf_op jit(solution)/shard_map/while/body/eval_jaxpr/ppermute | solution.py:19
  213.6 1.6 collective-permute-done.1
  215.5 2.6 %fusion.117 = f32[2,2,72,1024]{3,2,1,0:T(8,128)S(1)} fusion(f32[2,2,72,1024]{3,2,1,0:T(8,128)S(1)} %slice.1057, f32[4,2,8,1024]{3,2,1,0:T(8,128)S(1)} %collective-permute-done.1, f32[1,2,64,1024]{3,2,1,0:T(8,128)S(1)} %bitcast.94, f32[1,2,64,1024]{3,2,1,0:T(8,128)S(1)} %bitcast.85, f32[1,2,64,1024]{3,2,1,0:T(8,128)S(1)} %bitcast.91, ...), kind=kLoop, calls=%fused_computation.46.clone.1 | loop fusion | flops 8552448 | bytes 12058624 | tf_op jit(solution)/shard_map/while/body/eval_jaxpr/add | solution.py:36
  219.1 3.2 %fusion.118 = f32[2,72,1024]{2,1,0:T(8,128)S(1)} fusion(f32[2,2,72,1024]{3,2,1,0:T(8,128)S(1)} %fusion.117, f32[4,2,80,1024]{3,2,1,0:T(8,128)S(1)} %pad_maximum_fusion.23, s32[2,512]{1,0:T(2,128)S(1)} %copy-done.17, f32[72,1024]{1,0:T(8,128)S(1)} %bitcast.103, f32[72,1024]{1,0:T(8,128)S(1)} %bitcast.99, f32[2,512]{1,0:T(2,128)S(1)} %get-tuple-element.864, ...), kind=kOutput, calls=%fused_computation.109.clone.1 | convolution fusion | flops 909246464 | bytes 2961696 | tf_op jit(solution)/shard_map/while/body/eval_jaxpr/szr,srx->szx/dot_general | solution.py:81
  222.4 2.4 fusion.121
  226.1 3.1 %fusion.122 = f32[2,64,1024]{2,1,0:T(8,128)S(1)} fusion(s32[2,512]{1,0:T(2,128)S(1)} %copy-done.17, f32[2,2,64,1024]{3,2,1,0:T(8,128)S(1)} %fusion.121, f32[2,64,1024]{2,1,0:T(8,128)S(1)} %get-tuple-element.904, f32[2,64,1024]{2,1,0:T(8,128)S(1)} %get-tuple-element.927, f32[64,1024]{1,0:T(8,128)S(1)} %copy-done.12, ...), kind=kOutput, calls=%fused_computation.39.clone.1 | convolution fusion | flops 808452096 | bytes 2633984 | tf_op jit(solution)/shard_map/while/body/eval_jaxpr/szr,srx->szx/dot_general | solution.py:81
  230.2 19.8 %all-gather.3.cloned.1.call-done = f32[256,1024]{1,0:T(8,128)} async-done(((f32[64,1024]{1,0:T(8,128)}), f32[256,1024]{1,0:T(8,128)}) %all-gather.3.cloned.1.call-update) | async-done | bytes 1048592 | tf_op jit(solution)/shard_map/all_gather | solution.py:144
  (387 shorter events, 78.4 us)
Async XLA Ops:
  7.2 242.8 %all-gather.3.cloned.1.call-start = ((), (), s32[]{:S(2)}) async-start(), calls=%async_computation | async-start | bytes 1310720 | tf_op jit(solution)/shard_map/all_gather | solution.py:144
  7.2 1.7 copy-start.7
  7.2 8.2 %copy-start.13 = (f32[2,16,512]{2,1,0:T(8,128)S(1)}, f32[2,16,512]{2,1,0:T(8,128)}, u32[]{:S(2)}) copy-start(f32[2,16,512]{2,1,0:T(8,128)} %param.21) | copy-start | bytes 196612
  8.2 12.9 %copy-start.6 = (f32[2,64,1024]{2,1,0:T(8,128)S(1)}, f32[2,64,1024]{2,1,0:T(8,128)}, u32[]{:S(2)}) copy-start(f32[2,64,1024]{2,1,0:T(8,128)} %param.19) | copy-start | bytes 1572868
  8.9 12.1 %copy-start = (f32[256]{0:T(256)S(1)}, f32[256]{0:T(256)}, u32[]{:S(2)}) copy-start(f32[256]{0:T(256)} %param.22) | copy-start | bytes 3076
  8.9 12.1 %copy-start.1 = (f32[2,64,1024]{2,1,0:T(8,128)S(1)}, f32[2,64,1024]{2,1,0:T(8,128)}, u32[]{:S(2)}) copy-start(f32[2,64,1024]{2,1,0:T(8,128)} %param.17) | copy-start | bytes 1572868
  8.9 12.1 %copy-start.3 = (f32[2,64,1024]{2,1,0:T(8,128)S(1)}, f32[2,64,1024]{2,1,0:T(8,128)}, u32[]{:S(2)}) copy-start(f32[2,64,1024]{2,1,0:T(8,128)} %param.18) | copy-start | bytes 1572868
  8.9 12.1 %copy-start.5 = (f32[2,64,1024]{2,1,0:T(8,128)S(1)}, f32[2,64,1024]{2,1,0:T(8,128)}, u32[]{:S(2)}) copy-start(f32[2,64,1024]{2,1,0:T(8,128)} %param.20) | copy-start | bytes 1572868
  8.9 12.1 %copy-start.14 = (s32[2]{0:T(128)S(1)}, s32[2]{0:T(128)}, u32[]{:S(2)}) copy-start(s32[2]{0:T(128)} %param.27) | copy-start | bytes 28
  8.9 12.1 %copy-start.15 = (s32[2]{0:T(128)S(1)}, s32[2]{0:T(128)}, u32[]{:S(2)}) copy-start(s32[2]{0:T(128)} %param.24) | copy-start | bytes 28
  8.9 12.1 %copy-start.16 = (s32[2,512]{1,0:T(2,128)S(1)}, s32[2,512]{1,0:T(2,128)}, u32[]{:S(2)}) copy-start(s32[2,512]{1,0:T(2,128)} %param.25) | copy-start | bytes 12292
  9.0 12.1 %copy-start.18 = (s32[2]{0:T(128)S(1)}, s32[2]{0:T(128)}, u32[]{:S(2)}) copy-start(s32[2]{0:T(128)} %param.23) | copy-start | bytes 28
  9.0 7.0 %collective-permute-start.2 = (f32[2,8,1024]{2,1,0:T(8,128)S(1)}, f32[2,8,1024]{2,1,0:T(8,128)S(1)}, u32[]{:S(2)}, u32[]{:S(2)}) collective-permute-start(f32[2,8,1024]{2,1,0:T(8,128)S(1)} %get-tuple-element.729), channel_id=1, source_target_pairs={{0,1},{1,2},{2,3},{4,5},{5,6},{6,7},{8,9},{9,10},{10,11},{12,13},{... | collective-permute-start | bytes 196616 | tf_op jit(solution)/shard_map/ppermute | solution.py:19
  14.1 6.2 %collective-permute-start.3 = (f32[2,8,1024]{2,1,0:T(8,128)S(1)}, f32[2,8,1024]{2,1,0:T(8,128)S(1)}, u32[]{:S(2)}, u32[]{:S(2)}) collective-permute-start(f32[2,8,1024]{2,1,0:T(8,128)S(1)} %get-tuple-element.730), channel_id=1, source_target_pairs={{1,0},{2,1},{3,2},{5,4},{6,5},{7,6},{9,8},{10,9},{11,10},{13,12},{... | collective-permute-start | bytes 196616 | tf_op jit(solution)/shard_map/ppermute | solution.py:21
  21.9 8.7 %collective-permute-start = (f32[4,2,8,1024]{3,2,1,0:T(8,128)}, f32[4,2,8,1024]{3,2,1,0:T(8,128)S(1)}, u32[]{:S(2)}, u32[]{:S(2)}) collective-permute-start(f32[4,2,8,1024]{3,2,1,0:T(8,128)} %get-tuple-element.862), channel_id=1, source_target_pairs={{1,0},{2,1},{3,2},{5,4},{6,5},{7,6},{9,8},{10,9},{11,10},{13,12},{... | collective-permute-start | bytes 786440 | tf_op jit(solution)/shard_map/while/body/eval_jaxpr/ppermute | solution.py:21
  23.2 8.7 %collective-permute-start.1 = (f32[4,2,8,1024]{3,2,1,0:T(8,128)}, f32[4,2,8,1024]{3,2,1,0:T(8,128)S(1)}, u32[]{:S(2)}, u32[]{:S(2)}) collective-permute-start(f32[4,2,8,1024]{3,2,1,0:T(8,128)} %get-tuple-element.863), channel_id=1, source_target_pairs={{0,1},{1,2},{2,3},{4,5},{5,6},{6,7},{8,9},{9,10},{10,11},{12,13},{... | collective-permute-start | bytes 786440 | tf_op jit(solution)/shard_map/while/body/eval_jaxpr/ppermute | solution.py:19
  42.9 3.1 %copy-start.8 = (f32[64,1024]{1,0:T(8,128)S(1)}, f32[64,1024]{1,0:T(8,128)}, u32[]{:S(2)}) copy-start(f32[64,1024]{1,0:T(8,128)} %get-tuple-element.905) | copy-start | bytes 786436 | tf_op jit(solution)/shard_map/while
  42.9 4.0 %copy-start.19 = (s32[2]{0:T(128)S(1)}, s32[2]{0:T(128)}, u32[]{:S(2)}) copy-start(s32[2]{0:T(128)} %get-tuple-element.982) | copy-start | bytes 28 | tf_op jit(solution)/shard_map/while
  47.8 8.8 %collective-permute-start = (f32[4,2,8,1024]{3,2,1,0:T(8,128)}, f32[4,2,8,1024]{3,2,1,0:T(8,128)S(1)}, u32[]{:S(2)}, u32[]{:S(2)}) collective-permute-start(f32[4,2,8,1024]{3,2,1,0:T(8,128)} %get-tuple-element.862), channel_id=1, source_target_pairs={{1,0},{2,1},{3,2},{5,4},{6,5},{7,6},{9,8},{10,9},{11,10},{13,12},{... | collective-permute-start | bytes 786440 | tf_op jit(solution)/shard_map/while/body/eval_jaxpr/ppermute | solution.py:21
  49.0 9.1 %collective-permute-start.1 = (f32[4,2,8,1024]{3,2,1,0:T(8,128)}, f32[4,2,8,1024]{3,2,1,0:T(8,128)S(1)}, u32[]{:S(2)}, u32[]{:S(2)}) collective-permute-start(f32[4,2,8,1024]{3,2,1,0:T(8,128)} %get-tuple-element.863), channel_id=1, source_target_pairs={{0,1},{1,2},{2,3},{4,5},{5,6},{6,7},{8,9},{9,10},{10,11},{12,13},{... | collective-permute-start | bytes 786440 | tf_op jit(solution)/shard_map/while/body/eval_jaxpr/ppermute | solution.py:19
  69.1 3.1 %copy-start.8 = (f32[64,1024]{1,0:T(8,128)S(1)}, f32[64,1024]{1,0:T(8,128)}, u32[]{:S(2)}) copy-start(f32[64,1024]{1,0:T(8,128)} %get-tuple-element.905) | copy-start | bytes 786436 | tf_op jit(solution)/shard_map/while
  69.1 4.0 %copy-start.19 = (s32[2]{0:T(128)S(1)}, s32[2]{0:T(128)}, u32[]{:S(2)}) copy-start(s32[2]{0:T(128)} %get-tuple-element.982) | copy-start | bytes 28 | tf_op jit(solution)/shard_map/while
  73.9 8.8 %collective-permute-start = (f32[4,2,8,1024]{3,2,1,0:T(8,128)}, f32[4,2,8,1024]{3,2,1,0:T(8,128)S(1)}, u32[]{:S(2)}, u32[]{:S(2)}) collective-permute-start(f32[4,2,8,1024]{3,2,1,0:T(8,128)} %get-tuple-element.862), channel_id=1, source_target_pairs={{1,0},{2,1},{3,2},{5,4},{6,5},{7,6},{9,8},{10,9},{11,10},{13,12},{... | collective-permute-start | bytes 786440 | tf_op jit(solution)/shard_map/while/body/eval_jaxpr/ppermute | solution.py:21
  75.2 9.1 %collective-permute-start.1 = (f32[4,2,8,1024]{3,2,1,0:T(8,128)}, f32[4,2,8,1024]{3,2,1,0:T(8,128)S(1)}, u32[]{:S(2)}, u32[]{:S(2)}) collective-permute-start(f32[4,2,8,1024]{3,2,1,0:T(8,128)} %get-tuple-element.863), channel_id=1, source_target_pairs={{0,1},{1,2},{2,3},{4,5},{5,6},{6,7},{8,9},{9,10},{10,11},{12,13},{... | collective-permute-start | bytes 786440 | tf_op jit(solution)/shard_map/while/body/eval_jaxpr/ppermute | solution.py:19
  95.2 3.1 %copy-start.8 = (f32[64,1024]{1,0:T(8,128)S(1)}, f32[64,1024]{1,0:T(8,128)}, u32[]{:S(2)}) copy-start(f32[64,1024]{1,0:T(8,128)} %get-tuple-element.905) | copy-start | bytes 786436 | tf_op jit(solution)/shard_map/while
  95.2 4.0 %copy-start.19 = (s32[2]{0:T(128)S(1)}, s32[2]{0:T(128)}, u32[]{:S(2)}) copy-start(s32[2]{0:T(128)} %get-tuple-element.982) | copy-start | bytes 28 | tf_op jit(solution)/shard_map/while
  100.1 8.8 %collective-permute-start = (f32[4,2,8,1024]{3,2,1,0:T(8,128)}, f32[4,2,8,1024]{3,2,1,0:T(8,128)S(1)}, u32[]{:S(2)}, u32[]{:S(2)}) collective-permute-start(f32[4,2,8,1024]{3,2,1,0:T(8,128)} %get-tuple-element.862), channel_id=1, source_target_pairs={{1,0},{2,1},{3,2},{5,4},{6,5},{7,6},{9,8},{10,9},{11,10},{13,12},{... | collective-permute-start | bytes 786440 | tf_op jit(solution)/shard_map/while/body/eval_jaxpr/ppermute | solution.py:21
  101.4 9.1 %collective-permute-start.1 = (f32[4,2,8,1024]{3,2,1,0:T(8,128)}, f32[4,2,8,1024]{3,2,1,0:T(8,128)S(1)}, u32[]{:S(2)}, u32[]{:S(2)}) collective-permute-start(f32[4,2,8,1024]{3,2,1,0:T(8,128)} %get-tuple-element.863), channel_id=1, source_target_pairs={{0,1},{1,2},{2,3},{4,5},{5,6},{6,7},{8,9},{9,10},{10,11},{12,13},{... | collective-permute-start | bytes 786440 | tf_op jit(solution)/shard_map/while/body/eval_jaxpr/ppermute | solution.py:19
  121.4 3.1 %copy-start.8 = (f32[64,1024]{1,0:T(8,128)S(1)}, f32[64,1024]{1,0:T(8,128)}, u32[]{:S(2)}) copy-start(f32[64,1024]{1,0:T(8,128)} %get-tuple-element.905) | copy-start | bytes 786436 | tf_op jit(solution)/shard_map/while
  121.4 4.0 %copy-start.19 = (s32[2]{0:T(128)S(1)}, s32[2]{0:T(128)}, u32[]{:S(2)}) copy-start(s32[2]{0:T(128)} %get-tuple-element.982) | copy-start | bytes 28 | tf_op jit(solution)/shard_map/while
  126.3 8.8 %collective-permute-start = (f32[4,2,8,1024]{3,2,1,0:T(8,128)}, f32[4,2,8,1024]{3,2,1,0:T(8,128)S(1)}, u32[]{:S(2)}, u32[]{:S(2)}) collective-permute-start(f32[4,2,8,1024]{3,2,1,0:T(8,128)} %get-tuple-element.862), channel_id=1, source_target_pairs={{1,0},{2,1},{3,2},{5,4},{6,5},{7,6},{9,8},{10,9},{11,10},{13,12},{... | collective-permute-start | bytes 786440 | tf_op jit(solution)/shard_map/while/body/eval_jaxpr/ppermute | solution.py:21
  127.6 9.1 %collective-permute-start.1 = (f32[4,2,8,1024]{3,2,1,0:T(8,128)}, f32[4,2,8,1024]{3,2,1,0:T(8,128)S(1)}, u32[]{:S(2)}, u32[]{:S(2)}) collective-permute-start(f32[4,2,8,1024]{3,2,1,0:T(8,128)} %get-tuple-element.863), channel_id=1, source_target_pairs={{0,1},{1,2},{2,3},{4,5},{5,6},{6,7},{8,9},{9,10},{10,11},{12,13},{... | collective-permute-start | bytes 786440 | tf_op jit(solution)/shard_map/while/body/eval_jaxpr/ppermute | solution.py:19
  147.6 3.1 %copy-start.8 = (f32[64,1024]{1,0:T(8,128)S(1)}, f32[64,1024]{1,0:T(8,128)}, u32[]{:S(2)}) copy-start(f32[64,1024]{1,0:T(8,128)} %get-tuple-element.905) | copy-start | bytes 786436 | tf_op jit(solution)/shard_map/while
  147.6 4.0 %copy-start.19 = (s32[2]{0:T(128)S(1)}, s32[2]{0:T(128)}, u32[]{:S(2)}) copy-start(s32[2]{0:T(128)} %get-tuple-element.982) | copy-start | bytes 28 | tf_op jit(solution)/shard_map/while
  152.4 8.8 %collective-permute-start = (f32[4,2,8,1024]{3,2,1,0:T(8,128)}, f32[4,2,8,1024]{3,2,1,0:T(8,128)S(1)}, u32[]{:S(2)}, u32[]{:S(2)}) collective-permute-start(f32[4,2,8,1024]{3,2,1,0:T(8,128)} %get-tuple-element.862), channel_id=1, source_target_pairs={{1,0},{2,1},{3,2},{5,4},{6,5},{7,6},{9,8},{10,9},{11,10},{13,12},{... | collective-permute-start | bytes 786440 | tf_op jit(solution)/shard_map/while/body/eval_jaxpr/ppermute | solution.py:21
  153.7 9.1 %collective-permute-start.1 = (f32[4,2,8,1024]{3,2,1,0:T(8,128)}, f32[4,2,8,1024]{3,2,1,0:T(8,128)S(1)}, u32[]{:S(2)}, u32[]{:S(2)}) collective-permute-start(f32[4,2,8,1024]{3,2,1,0:T(8,128)} %get-tuple-element.863), channel_id=1, source_target_pairs={{0,1},{1,2},{2,3},{4,5},{5,6},{6,7},{8,9},{9,10},{10,11},{12,13},{... | collective-permute-start | bytes 786440 | tf_op jit(solution)/shard_map/while/body/eval_jaxpr/ppermute | solution.py:19
  173.8 3.1 %copy-start.8 = (f32[64,1024]{1,0:T(8,128)S(1)}, f32[64,1024]{1,0:T(8,128)}, u32[]{:S(2)}) copy-start(f32[64,1024]{1,0:T(8,128)} %get-tuple-element.905) | copy-start | bytes 786436 | tf_op jit(solution)/shard_map/while
  173.8 4.0 %copy-start.19 = (s32[2]{0:T(128)S(1)}, s32[2]{0:T(128)}, u32[]{:S(2)}) copy-start(s32[2]{0:T(128)} %get-tuple-element.982) | copy-start | bytes 28 | tf_op jit(solution)/shard_map/while
  178.6 8.8 %collective-permute-start = (f32[4,2,8,1024]{3,2,1,0:T(8,128)}, f32[4,2,8,1024]{3,2,1,0:T(8,128)S(1)}, u32[]{:S(2)}, u32[]{:S(2)}) collective-permute-start(f32[4,2,8,1024]{3,2,1,0:T(8,128)} %get-tuple-element.862), channel_id=1, source_target_pairs={{1,0},{2,1},{3,2},{5,4},{6,5},{7,6},{9,8},{10,9},{11,10},{13,12},{... | collective-permute-start | bytes 786440 | tf_op jit(solution)/shard_map/while/body/eval_jaxpr/ppermute | solution.py:21
  179.9 9.1 %collective-permute-start.1 = (f32[4,2,8,1024]{3,2,1,0:T(8,128)}, f32[4,2,8,1024]{3,2,1,0:T(8,128)S(1)}, u32[]{:S(2)}, u32[]{:S(2)}) collective-permute-start(f32[4,2,8,1024]{3,2,1,0:T(8,128)} %get-tuple-element.863), channel_id=1, source_target_pairs={{0,1},{1,2},{2,3},{4,5},{5,6},{6,7},{8,9},{9,10},{10,11},{12,13},{... | collective-permute-start | bytes 786440 | tf_op jit(solution)/shard_map/while/body/eval_jaxpr/ppermute | solution.py:19
  199.9 3.1 %copy-start.8 = (f32[64,1024]{1,0:T(8,128)S(1)}, f32[64,1024]{1,0:T(8,128)}, u32[]{:S(2)}) copy-start(f32[64,1024]{1,0:T(8,128)} %get-tuple-element.905) | copy-start | bytes 786436 | tf_op jit(solution)/shard_map/while
  199.9 4.0 %copy-start.19 = (s32[2]{0:T(128)S(1)}, s32[2]{0:T(128)}, u32[]{:S(2)}) copy-start(s32[2]{0:T(128)} %get-tuple-element.982) | copy-start | bytes 28 | tf_op jit(solution)/shard_map/while
  204.8 8.8 %collective-permute-start = (f32[4,2,8,1024]{3,2,1,0:T(8,128)}, f32[4,2,8,1024]{3,2,1,0:T(8,128)S(1)}, u32[]{:S(2)}, u32[]{:S(2)}) collective-permute-start(f32[4,2,8,1024]{3,2,1,0:T(8,128)} %get-tuple-element.862), channel_id=1, source_target_pairs={{1,0},{2,1},{3,2},{5,4},{6,5},{7,6},{9,8},{10,9},{11,10},{13,12},{... | collective-permute-start | bytes 786440 | tf_op jit(solution)/shard_map/while/body/eval_jaxpr/ppermute | solution.py:21
  206.1 9.1 %collective-permute-start.1 = (f32[4,2,8,1024]{3,2,1,0:T(8,128)}, f32[4,2,8,1024]{3,2,1,0:T(8,128)S(1)}, u32[]{:S(2)}, u32[]{:S(2)}) collective-permute-start(f32[4,2,8,1024]{3,2,1,0:T(8,128)} %get-tuple-element.863), channel_id=1, source_target_pairs={{0,1},{1,2},{2,3},{4,5},{5,6},{6,7},{8,9},{9,10},{10,11},{12,13},{... | collective-permute-start | bytes 786440 | tf_op jit(solution)/shard_map/while/body/eval_jaxpr/ppermute | solution.py:19
  226.1 3.1 %copy-start.8 = (f32[64,1024]{1,0:T(8,128)S(1)}, f32[64,1024]{1,0:T(8,128)}, u32[]{:S(2)}) copy-start(f32[64,1024]{1,0:T(8,128)} %get-tuple-element.905) | copy-start | bytes 786436 | tf_op jit(solution)/shard_map/while
  226.1 4.0 %copy-start.19 = (s32[2]{0:T(128)S(1)}, s32[2]{0:T(128)}, u32[]{:S(2)}) copy-start(s32[2]{0:T(128)} %get-tuple-element.982) | copy-start | bytes 28 | tf_op jit(solution)/shard_map/while
  230.1 21.9 %copy-start.2 = (f32[2,64,1024]{2,1,0:T(8,128)}, f32[2,64,1024]{2,1,0:T(8,128)S(1)}, u32[]{:S(2)}) copy-start(f32[2,64,1024]{2,1,0:T(8,128)S(1)} %get-tuple-element.960) | copy-start | bytes 1572868
  230.1 21.9 %copy-start.4 = (f32[2,64,1024]{2,1,0:T(8,128)}, f32[2,64,1024]{2,1,0:T(8,128)S(1)}, u32[]{:S(2)}) copy-start(f32[2,64,1024]{2,1,0:T(8,128)S(1)} %get-tuple-element.962) | copy-start | bytes 1572868
  (65 other events, 53.8 us)
Sparse Core Ops, SparseCore 0:
  230.3 19.6 all-gather.2
